TPU v7x, 256 devices: a 8x8x2 block of a 8x8x16 slice. The times are simulated.
256 devices in a mesh: parts: 2 (over z), genes: 64 (over x, y), samples: 2 (over core).
Axes of the slice: x: 8, y: 8, z: 2, core: 2. Of those that a mesh axis runs over, the one named last changes fastest.
The devices are a block of a 8x8x16 slice.
Arguments:
- dosage: bfloat16 [262144, 2048], P(('parts', 'genes'), 'samples'), parts along dimension 0, may hold values from -6 to 6
- expression: bfloat16 [1024, 2048], P(('parts', 'genes'), 'samples'), parts along dimension 0, may hold values from -6 to 6
- intron_counts: bfloat16 [4096, 20480], P(('parts', 'samples', 'genes')), parts along dimension 0, may hold values from 1 to 100
- cluster_sizes: int32 [1024, 8], P('parts'), parts along dimension 0, may hold values from 1 to 12, 40 in all within a row
- valid_mask: int32 [1024, 40], P('parts'), parts along dimension 0, may hold values 0 or 1
- gene_block: int32 [1024], P('parts'), parts along dimension 0, may hold values from 0 to 511, each once
- window_start: int32 [1024], P(('parts', 'genes')), parts along dimension 0, may hold values from 0 to 1024, as said below
Outputs:
- assoc: bfloat16 [1024, 41, 2048], P(('parts', 'genes'), None, 'samples'), parts along dimension 0
There are 2 independent parts, one for each index of `parts`. A program takes and returns all parts, laid end to end along the dimension named above; each array names one. Nothing has to cross between parts.
Inputs may be any that keep to these rules, and one draw needn't show every extreme that they name: Every window_start is a multiple of 128 and at most 1024; some gene reaches 1024 in every draw. `gene_block`: a permutation of the genes. `cluster_sizes`: each row sums to 40.
All inputs are finite; a program needn't handle non-finite values.
Results may differ from a plain program's by a relative error of at most 0.0058.
Values may be sent and summed in bfloat16 or wider, within the bound.
A program may use at most 64 MiB of HBM per device.

v0:
```python
import jax
import jax.numpy as jnp
from jax import lax
from jax.sharding import PartitionSpec as P

W = 2048
SLOTS = 40
SPILL = 1024
ALIGN = 128
PHEN = 41


def shifted(block, axis, distance):
    devices = range(lax.axis_size(axis))
    route = [(i - distance, i) for i in devices if i - distance in devices]
    return lax.ppermute(block, axis, route)


def together(arrays, axis):
    vector, at, finished = (jnp.concatenate([a.reshape(-1) for a in arrays]), 0, [])
    subtotal = lax.psum(vector, axis)
    for a in arrays:
        finished.append(subtotal[at : at + a.size].reshape(a.shape))
        at += a.size
    return tuple(finished)


def in_blocks(x, dim, count):
    shape = x.shape
    parts = x.reshape(*shape[:dim], count, shape[dim] // count, *shape[dim + 1 :])
    return jnp.moveaxis(parts, dim, 0)


def summed_on_arrival(x, axis, dim):
    count = lax.axis_size(axis)
    parts = lax.all_to_all(in_blocks(x, dim, count), axis, 0, 0, tiled=True)
    return jnp.sum(parts, axis=0)


def cluster_ratios(counts, cluster_sizes, valid_mask):
    cluster_ends = jnp.cumsum(cluster_sizes, axis=1, dtype=jnp.int32)
    slot_index = jnp.arange(SLOTS, dtype=jnp.int32)
    cluster_id = jnp.sum(
        (cluster_ends[:, None, :] <= slot_index[None, :, None]).astype(jnp.int32),
        axis=2,
        dtype=jnp.int32,
    )
    same_cluster = (cluster_id[:, :, None] == cluster_id[:, None, :]).astype(jnp.float32)
    live_counts = counts * valid_mask.astype(jnp.float32)[None, :, :]
    cluster_total = jnp.einsum(
        "sgj,gjk->sgk", live_counts, same_cluster, precision=lax.Precision.HIGHEST
    )
    return (live_counts / jnp.maximum(cluster_total, 1.0)).astype(jnp.bfloat16)


def tile_window(owner_block, offset, width):
    leading = owner_block.shape[:-1]
    tiles = owner_block.reshape(leading + (owner_block.shape[-1] // ALIGN, ALIGN))
    first_tile = offset // ALIGN
    piece = lax.dynamic_slice_in_dim(tiles, first_tile, width // ALIGN, len(leading))
    return piece.reshape(leading + (width,))


def window_slices(product, row_sum, row_square, starts, width):

    def window_of(owner_block, offset):
        return tile_window(owner_block, offset, width)

    cross_part = jax.vmap(window_of, in_axes=(0, 0))(product, starts)
    sum_part = jax.vmap(window_of, in_axes=(None, 0))(row_sum, starts)
    square_part = jax.vmap(window_of, in_axes=(None, 0))(row_square, starts)
    return (cross_part, sum_part, square_part)


def finish_stats(cross_part, sum_part, square_part, phen_sum, phen_square, sample_count):
    numerator = cross_part - sum_part[:, None, :] * phen_sum[:, :, None] / sample_count
    dose_var = jnp.maximum(square_part - sum_part * sum_part / sample_count, 1.0)
    pheno_var = jnp.maximum(phen_square - phen_sum * phen_sum / sample_count, 1.0)
    return (numerator * lax.rsqrt(dose_var)[:, None, :] * lax.rsqrt(pheno_var)[:, :, None]).astype(
        jnp.bfloat16
    )


def shards(dosage, expression, intron_counts, cluster_sizes, valid_mask, gene_block, window_start):
    samp_dev = dosage.shape[1]
    gene_dev = expression.shape[0]
    total_genes = gene_block.shape[0]
    next_rows = shifted(dosage[:SPILL], "genes", -1)
    dose_rows = jnp.concatenate([dosage, next_rows], axis=0)
    stored = intron_counts.reshape(intron_counts.shape[0], total_genes, SLOTS)
    counts = jnp.take(stored, gene_block, axis=1).astype(jnp.float32)
    ratios = cluster_ratios(counts, cluster_sizes, valid_mask).reshape(
        intron_counts.shape[0], total_genes * SLOTS
    )
    exchanged = lax.all_to_all(ratios, "genes", split_axis=1, concat_axis=0, tiled=True)
    intron_panel = exchanged.reshape(samp_dev, gene_dev, SLOTS)
    n_samples = lax.axis_size("samples")
    half_width = W // n_samples
    offset = lax.axis_index("samples") * half_width
    contract = (((0,), (1,)), ((), ()))
    pheno_panel = jnp.concatenate([expression.T[:, :, None], intron_panel], axis=2).reshape(
        samp_dev, gene_dev * PHEN
    )
    product = lax.dot_general(pheno_panel, dose_rows, contract, preferred_element_type=jnp.float32)
    product = product.reshape(gene_dev, PHEN, W + SPILL)
    pheno_float = pheno_panel.astype(jnp.float32)
    phen_sum = jnp.sum(pheno_float, axis=0).reshape(gene_dev, PHEN)
    phen_square = jnp.sum(pheno_float * pheno_float, axis=0).reshape(gene_dev, PHEN)
    dose_float = dose_rows.astype(jnp.float32)
    row_sum = jnp.sum(dose_float, axis=1)
    row_square = jnp.sum(dose_float * dose_float, axis=1)
    row_sum, row_square, phen_sum, phen_square = together(
        (row_sum, row_square, phen_sum, phen_square), "samples"
    )
    cross_part, sum_part, square_part = window_slices(product, row_sum, row_square, window_start, W)
    cross_sums = summed_on_arrival(cross_part, "samples", 2)
    sum_half = lax.dynamic_slice_in_dim(sum_part, offset, half_width, 1)
    square_half = lax.dynamic_slice_in_dim(square_part, offset, half_width, 1)
    sample_count = float(samp_dev * n_samples)
    return finish_stats(cross_sums, sum_half, square_half, phen_sum, phen_square, sample_count)


def solution(mesh):
    in_specs = (
        P(("parts", "genes"), "samples"),
        P(("parts", "genes"), "samples"),
        P(("parts", "samples", "genes"), None),
        P("parts", None),
        P("parts", None),
        P("parts"),
        P(("parts", "genes")),
    )
    out_specs = P(("parts", "genes"), None, "samples")
    return jax.shard_map(shards, mesh=mesh, in_specs=in_specs, out_specs=out_specs, check_vma=False)
```

profile of v0, /device:TPU:515, one launch (start us, length us, event | category | flops | bytes accessed | tf_op | source)
XLA Modules:
  0.0 155.1 jit_solution(954485686904478293)
XLA Ops:
  0.0 3.1 %slice.15 = bf16[1024,1024]{1,0:T(8,128)(2,1)} slice(bf16[2048,1024]{1,0:T(8,128)(2,1)} %param.7), slice={[0:1024], [0:1024]} | slice | bytes 4194304 | tf_op jit(solution)/shard_map/slice | solution.py:88
  3.1 13.4 %collective-permute-start = (bf16[1024,1024]{1,0:T(8,128)(2,1)}, bf16[1024,1024]{1,0:T(8,128)(2,1)}, u32[]{:S(2)}, u32[]{:S(2)}) collective-permute-start(bf16[1024,1024]{1,0:T(8,128)(2,1)} %slice.15), channel_id=1, source_target_pairs={{2,0},{4,2},{6,4},{8,6},{10,8},{12,10},{14,12},{16,14},{18,16},{20... | collective-permute-start | bytes 6291464 | tf_op jit(solution)/shard_map/ppermute | solution.py:16
  16.5 4.9 %reshape.65 = bf16[16,512,40]{2,1,0:T(8,128)(2,1)} reshape(bf16[16,20480]{1,0:T(8,128)(2,1)S(1)} %copy-done) | data formatting | bytes 1310720 | tf_op jit(solution)/shard_map/reshape | solution.py:90
  21.4 2.9 %copy.89 = bf16[16,512,40]{2,0,1:T(8,128)(2,1)S(1)} copy(bf16[16,512,40]{2,1,0:T(8,128)(2,1)} %reshape.65) | data formatting | bytes 1310720 | tf_op jit(solution)/shard_map/reshape | solution.py:90
  24.4 2.8 %gather_fusion = bf16[512,16,40]{2,1,0:T(8,128)(2,1)} fusion(bf16[16,512,40]{2,0,1:T(8,128)(2,1)S(1)} %copy.89, s32[1024]{0:T(1024)S(1)} %pad_clamp_fusion), kind=kCustom, calls=%fused_computation | custom fusion | bytes 1312768 | tf_op jit(solution)/shard_map/jit(_take)/gather | solution.py:91
  27.2 2.5 %copy.90 = bf16[512,16,40]{0,2,1:T(8,128)(2,1)S(1)} copy(bf16[512,16,40]{2,1,0:T(8,128)(2,1)} %gather_fusion) | data formatting | bytes 1310720 | tf_op jit(solution)/shard_map/jit(_take)/gather | solution.py:91
  29.9 3.7 %copy.93 = f32[16,512,40]{2,0,1:T(8,128)} copy(f32[16,512,40]{1,2,0:T(8,128)S(1)} %multiply_bitcast_fusion) | data formatting | bytes 2621440 | tf_op jit(solution)/shard_map/mul | solution.py:49
  34.0 10.0 %fusion.1 = f32[512,40,16]{1,2,0:T(8,128)} fusion(f32[16,512,40]{2,0,1:T(8,128)} %copy.93, s32[512,40]{1,0:T(8,128)S(1)} %copy.91), kind=kOutput, calls=%fused_computation.9 | convolution fusion | flops 158105600 | bytes 2703360 | tf_op jit(solution)/shard_map/sgj,gjk->sgk/dot_general | solution.py:50
  44.0 2.8 %copy.94 = f32[512,40,16]{0,1,2:T(8,128)S(1)} copy(f32[512,40,16]{1,2,0:T(8,128)} %fusion.1) | data formatting | bytes 2621440 | tf_op jit(solution)/shard_map/sgj,gjk->sgk/dot_general | solution.py:50
  47.1 1.1 copy.95
  48.2 1.4 all_to_all.15
  49.6 1.4 copy.96
  51.0 8.7 %all-to-all-start = ((bf16[16,64,320]{2,0,1:T(8,128)(2,1)}), bf16[16,64,320]{2,0,1:T(8,128)(2,1)S(1)}, u32[]{:S(2)}, u32[]{:S(2)}) async-start(bf16[16,64,320]{2,0,1:T(8,128)(2,1)} %copy.96), calls=%async_computation | async-start | bytes 1572864 | tf_op jit(solution)/shard_map/all_to_all | solution.py:95
  59.7 4.6 %constant_dynamic-update-slice_fusion.1 = bf16[3072,1024]{1,0:T(8,128)(2,1)} fusion(bf16[2048,1024]{1,0:T(8,128)(2,1)} %param.7), kind=kLoop, calls=%fused_computation.34 | loop fusion | bytes 8388608
  64.3 19.8 %all-to-all-done = bf16[16,64,320]{2,0,1:T(8,128)(2,1)S(1)} async-done(((bf16[16,64,320]{2,0,1:T(8,128)(2,1)}), bf16[16,64,320]{2,0,1:T(8,128)(2,1)S(1)}, u32[]{:S(2)}, u32[]{:S(2)}) %all-to-all-start) | async-done | bytes 655392 | tf_op jit(solution)/shard_map/all_to_all | solution.py:95
  84.0 1.8 %reshape.66 = bf16[1024,8,40]{2,1,0:T(8,128)(2,1)S(1)} reshape(bf16[64,16,320]{2,1,0:T(8,128)(2,1)S(1)} %bitcast.58) | data formatting | bytes 1310720 | tf_op jit(solution)/shard_map/reshape | solution.py:96
  85.8 2.1 %copy.97 = bf16[1024,8,40]{0,1,2:T(8,128)(2,1)S(1)} copy(bf16[1024,8,40]{2,1,0:T(8,128)(2,1)S(1)} %reshape.66) | data formatting | bytes 1310720 | tf_op jit(solution)/shard_map/reshape | solution.py:96
  89.4 3.1 %constant_dynamic-update-slice_fusion = bf16[3072,1024]{1,0:T(8,128)(2,1)} fusion(bf16[3072,1024]{1,0:T(8,128)(2,1)} %constant_dynamic-update-slice_fusion.1, bf16[1024,1024]{1,0:T(8,128)(2,1)} %collective-permute-done), kind=kLoop, calls=%fused_computation.33 | loop fusion | bytes 4194304 | tf_op jit(solution)/shard_map/concatenate | solution.py:89
  92.5 4.7 %fusion = (f32[3072]{0:T(1024)S(1)}, f32[3072]{0:T(1024)S(1)}) fusion(bf16[3072,1024]{1,0:T(8,128)(2,1)} %constant_dynamic-update-slice_fusion), kind=kLoop, calls=%fused_computation.8 | loop fusion | flops 12576768 | bytes 6316032 | tf_op jit(solution)/shard_map/reduce_sum | solution.py:111
  97.2 7.0 %psum.7 = f32[6800]{0:T(1024)S(1)} all-reduce(f32[6800]{0:T(1024)S(1)} %concatenate.19), channel_id=1, replica_groups=mesh['parts'=2,'genes'=64,'samples'=2] {'samples'}, use_global_device_ids=true, to_apply=%region_7.8 | all-reduce | flops 6800 | bytes 54400 | tf_op jit(solution)/shard_map/psum | solution.py:21
  104.3 9.6 %while.2 = (s32[]{:T(128)}, f32[24,128]{1,0:T(8,128)S(1)}, s32[8,2]{0,1:T(2,128)S(1)}, f32[8,16,128]{2,1,0:T(8,128)S(1)}, s32[]{:T(128)}) while((s32[]{:T(128)}, f32[24,128]{1,0:T(8,128)S(1)}, s32[8,2]{0,1:T(2,128)S(1)}, f32[8,16,128]{2,1,0:T(8,128)S(1)}, s32[]{:T(128)}) %tuple.36), condition=%wide.while_cond, body=%wide.while_body.sunk | while | flops 2 | bytes 16481 | solution.py:60
  104.9 0.6 bitcast_dynamic-update-slice_fusion.4
  106.1 0.6 bitcast_dynamic-update-slice_fusion.4
  107.3 0.6 bitcast_dynamic-update-slice_fusion.4
  108.5 0.6 bitcast_dynamic-update-slice_fusion.4
  109.7 0.6 bitcast_dynamic-update-slice_fusion.4
  110.9 0.6 bitcast_dynamic-update-slice_fusion.4
  112.1 0.6 bitcast_dynamic-update-slice_fusion.4
  113.3 0.6 bitcast_dynamic-update-slice_fusion.4
  113.9 9.6 %while.3 = (s32[]{:T(128)}, f32[24,128]{1,0:T(8,128)S(1)}, s32[8,2]{0,1:T(2,128)S(1)}, f32[8,16,128]{2,1,0:T(8,128)S(1)}, s32[]{:T(128)}) while((s32[]{:T(128)}, f32[24,128]{1,0:T(8,128)S(1)}, s32[8,2]{0,1:T(2,128)S(1)}, f32[8,16,128]{2,1,0:T(8,128)S(1)}, s32[]{:T(128)}) %tuple.39), condition=%wide.while_cond.1, body=%wide.while_body.1.sunk | while | flops 2 | bytes 16481 | solution.py:60
  114.5 0.6 bitcast_dynamic-update-slice_fusion.5
  115.7 0.6 bitcast_dynamic-update-slice_fusion.5
  116.9 0.6 bitcast_dynamic-update-slice_fusion.5
  118.1 0.6 bitcast_dynamic-update-slice_fusion.5
  119.3 0.6 bitcast_dynamic-update-slice_fusion.5
  120.5 0.6 bitcast_dynamic-update-slice_fusion.5
  121.7 0.6 bitcast_dynamic-update-slice_fusion.5
  122.9 0.6 bitcast_dynamic-update-slice_fusion.5
  123.6 8.7 %fusion.12 = f32[8,41,24,128]{3,1,0,2:T(8,128)} fusion(bf16[8,41,1024,1]{2,1,0,3:T(8,128)(2,1)S(1)} %reshape.127, bf16[24,128,1024,1]{2,1,3,0:T(8,128)(2,1)} %bitcast.56), kind=kOutput, calls=%fused_computation.46 | convolution fusion | flops 2063597568 | bytes 10993664 | tf_op jit(solution)/shard_map/dot_general | solution.py:104
  132.3 3.1 %gather_fusion.1 = f32[8,41,16,128]{3,1,2,0:T(8,128)S(1)} fusion(f32[8,41,24,128]{3,1,0,2:T(8,128)} %fusion.12, s32[8]{0:T(128)S(1)} %or_bitcast_fusion), kind=kCustom, calls=%fused_computation.1 | custom fusion | bytes 5374080 | tf_op jit(solution)/shard_map/vmap()/gather | solution.py:60
  135.4 2.3 %copy.100 = f32[8,41,16,128]{3,2,1,0:T(8,128)} copy(f32[8,41,16,128]{3,1,2,0:T(8,128)S(1)} %gather_fusion.1) | data formatting | bytes 5373952 | tf_op jit(solution)/shard_map/vmap()/gather | solution.py:60
  137.7 3.1 %reshape.68 = f32[8,41,2,1024]{3,2,1,0:T(2,128)S(1)} reshape(f32[8,41,16,128]{3,2,1,0:T(8,128)} %copy.100) | data formatting | bytes 5373952 | tf_op jit(solution)/shard_map/reshape;vmap()/reshape | solution.py:30
  140.8 2.3 %copy.101 = f32[2,8,41,1024]{3,1,2,0:T(8,128)} copy(f32[2,8,41,1024]{3,0,2,1:T(2,128)S(1)} %bitcast.57) | data formatting | bytes 5373952 | tf_op jit(solution)/shard_map/transpose | solution.py:31
  143.2 4.0 %all-to-all-start.1 = ((f32[2,8,41,1024]{3,1,2,0:T(8,128)}), f32[2,8,41,1024]{3,1,2,0:T(8,128)S(1)}, u32[]{:S(2)}, u32[]{:S(2)}) async-start(f32[2,8,41,1024]{3,1,2,0:T(8,128)} %copy.101), calls=%async_computation.1 | async-start | bytes 5373952 | tf_op jit(solution)/shard_map/all_to_all | solution.py:36
  147.3 2.8 %all-to-all-done.1 = f32[2,8,41,1024]{3,1,2,0:T(8,128)S(1)} async-done(((f32[2,8,41,1024]{3,1,2,0:T(8,128)}), f32[2,8,41,1024]{3,1,2,0:T(8,128)S(1)}, u32[]{:S(2)}, u32[]{:S(2)}) %all-to-all-start.1) | async-done | bytes 2687008 | tf_op jit(solution)/shard_map/all_to_all | solution.py:36
  150.2 1.4 reduce_sum.59
  151.6 2.3 %fusion.7 = bf16[8,41,1024]{2,1,0:T(8,128)(2,1)S(1)} fusion(f32[8,41,1024]{2,0,1:T(8,128)} %reduce_sum.59, f32[8,41]{1,0:T(8,128)S(1)} %maximum_rsqrt_fusion.1, f32[8,1024]{1,0:T(8,128)S(1)} %get-tuple-element.42, f32[8,41]{1,0:T(8,128)S(1)} %mul.65, f32[8,1024]{1,0:T(8,128)S(1)} %get-tuple-element.41), kind=kLoop, calls=%fused_computation.18 | loop fusion | flops 2015232 | bytes 2083392 | tf_op jit(solution)/shard_map/convert_element_type | solution.py:79
  153.9 1.2 copy.105
  (76 shorter events, 12.3 us)
Async XLA Ops:
  0.0 16.5 %copy-start.4 = (s32[512]{0:T(512)S(1)}, s32[512]{0:T(512)}, u32[]{:S(2)}) copy-start(s32[512]{0:T(512)} %param.12) | copy-start | bytes 6148
  0.0 16.5 %copy-start = (bf16[16,20480]{1,0:T(8,128)(2,1)S(1)}, bf16[16,20480]{1,0:T(8,128)(2,1)}, u32[]{:S(2)}) copy-start(bf16[16,20480]{1,0:T(8,128)(2,1)} %param.9) | copy-start | bytes 1966084
  3.1 86.3 %collective-permute-start = (bf16[1024,1024]{1,0:T(8,128)(2,1)}, bf16[1024,1024]{1,0:T(8,128)(2,1)}, u32[]{:S(2)}, u32[]{:S(2)}) collective-permute-start(bf16[1024,1024]{1,0:T(8,128)(2,1)} %slice.15), channel_id=1, source_target_pairs={{2,0},{4,2},{6,4},{8,6},{10,8},{12,10},{14,12},{16,14},{18,16},{20... | collective-permute-start | bytes 6291464 | tf_op jit(solution)/shard_map/ppermute | solution.py:16
  27.1 2.5 %copy-start.1 = (s32[512,40]{0,1:T(8,128)S(1)}, s32[512,40]{0,1:T(8,128)}, u32[]{:S(2)}) copy-start(s32[512,40]{0,1:T(8,128)} %param.11) | copy-start | bytes 245764
  29.9 3.7 %copy-start.3 = (s32[512,8]{0,1:T(8,128)S(1)}, s32[512,8]{0,1:T(8,128)}, u32[]{:S(2)}) copy-start(s32[512,8]{0,1:T(8,128)} %param.10) | copy-start | bytes 49156
  49.6 10.0 %copy-start.5 = (s32[8]{0:T(128)S(1)}, s32[8]{0:T(128)}, u32[]{:S(2)}) copy-start(s32[8]{0:T(128)} %param.13) | copy-start | bytes 100
  51.0 33.1 %all-to-all-start = ((bf16[16,64,320]{2,0,1:T(8,128)(2,1)}), bf16[16,64,320]{2,0,1:T(8,128)(2,1)S(1)}, u32[]{:S(2)}, u32[]{:S(2)}) async-start(bf16[16,64,320]{2,0,1:T(8,128)(2,1)} %copy.96), calls=%async_computation | async-start | bytes 1572864 | tf_op jit(solution)/shard_map/all_to_all | solution.py:95
  85.8 2.1 %copy-start.2 = (bf16[8,1024]{1,0:T(8,128)(2,1)S(1)}, bf16[8,1024]{1,0:T(8,128)(2,1)}, u32[]{:S(2)}) copy-start(bf16[8,1024]{1,0:T(8,128)(2,1)} %param.8) | copy-start | bytes 49156
  143.2 7.0 %all-to-all-start.1 = ((f32[2,8,41,1024]{3,1,2,0:T(8,128)}), f32[2,8,41,1024]{3,1,2,0:T(8,128)S(1)}, u32[]{:S(2)}, u32[]{:S(2)}) async-start(f32[2,8,41,1024]{3,1,2,0:T(8,128)} %copy.101), calls=%async_computation.1 | async-start | bytes 5373952 | tf_op jit(solution)/shard_map/all_to_all | solution.py:36
where the time goes:
time: 156 us; the launch traced here: 155 us
  local copies, waits for them, and re-layouts  70.6 us (45%)
  starting transfers between devices  26.1 us (17%)
  waiting for transfers between devices  22.6 us (14%)
  matrix products  18.7 us (12%)
  other arithmetic  9.51 us (6%)
  blocking collectives  6.96 us (4%)
    all_to_all x1, waiting for transfers between devices, shards(): lax.all_to_all(ratios, 'genes', split_axis=1, concat_axis=0, tiled=True)  19.8 us
    gather x48, local copies, waits for them, and re-layouts  18.8 us
    ppermute x1, starting transfers between devices, shifted(): return lax.ppermute(block, axis, route)  13.4 us
    dot_general x1, matrix products, cluster_ratios(): jnp.einsum('sgj,gjk->sgk', live_counts, same_cluster, precision=lax.Preci...  10 us
    all_to_all x1, starting transfers between devices, shards(): lax.all_to_all(ratios, 'genes', split_axis=1, concat_axis=0, tiled=True)  8.66 us
    dot_general x1, matrix products, shards(): lax.dot_general(pheno_panel, dose_rows, contract, preferred_element_type=...  8.66 us
    reshape x2, local copies, waits for them, and re-layouts, shards(): stored = intron_counts.reshape(intron_counts.shape[0], total_genes, SLOTS)  7.84 us
    psum x1, blocking collectives, together(): subtotal = lax.psum(vector, axis)  6.96 us
  transfers between devices with their start and end apart: 3, of which 2 were waited for; matrix products, arithmetic and copies ran while one was open for 28% of the time, Pallas kernels for 0%

commit v1 on v0

v1 whole, which is shorter than its diff:
```python
import functools

import jax
import jax.numpy as jnp
from jax import lax
from jax.experimental import pallas as pl
from jax.experimental.pallas import tpu as pltpu
from jax.sharding import PartitionSpec as P

W = 2048
HALF = 1024
SLOTS = 40
ALIGN = 128
PHEN = 41
ROWS = 48
GENE_DEV = 8
LANES = 384
SIDE = 8
MESH = pl.DeviceIdType.MESH
NT = (((1,), (1,)), ((), ()))


def permuted(counts_ref, block_ref, msgs_ref, owner):
    lane = lax.broadcasted_iota(jnp.int32, (16, ALIGN), 1)
    last = counts_ref.shape[1] // ALIGN - 2
    tiles = [jnp.zeros((16, ALIGN), jnp.float32) for _ in range(3)]
    for j in range(GENE_DEV):
        first = block_ref[owner * GENE_DEV + j] * SLOTS
        tile = jnp.minimum(first // ALIGN, last)
        start = first - tile * ALIGN
        at = pl.multiple_of(tile * ALIGN, ALIGN)
        a = counts_ref[:, pl.ds(at, ALIGN)].astype(jnp.float32)
        b = counts_ref[:, pl.ds(pl.multiple_of(at + ALIGN, ALIGN), ALIGN)].astype(jnp.float32)
        q = j * SLOTS % ALIGN
        turn = (q - start + 2 * ALIGN) % ALIGN
        a = pltpu.roll(a, turn, 1)
        b = pltpu.roll(b, turn, 1)
        index = (lane - q + ALIGN) % ALIGN
        gene = jnp.where(index + start < ALIGN, a, b)
        t = j * SLOTS // ALIGN
        tiles[t] = jnp.where((lane >= q) & (lane < q + SLOTS), gene, tiles[t])
        if q + SLOTS > ALIGN:
            tiles[t + 1] = jnp.where(lane < q + SLOTS - ALIGN, gene, tiles[t + 1])
    msgs_ref[owner] = jnp.concatenate(tiles, axis=1).astype(jnp.bfloat16)


def permute(block_ref, counts_ref, msgs_ref):
    @pl.loop(0, msgs_ref.shape[0])
    def _(owner):
        permuted(counts_ref, block_ref, msgs_ref, owner)


def kernel(
    n,
    msgs,
    expr_ref,
    keyl_ref,
    idxl_ref,
    keyr_ref,
    idxr_ref,
    dose_ref,
    z_ref,
    raw,
    expr,
    panel,
    dose,
    stat,
    pstat,
    sd,
    back,
    direct_sem,
    relay_sem,
    panel_sem,
    sent_sem,
    local_sem,
    dose_sem,
    expr_sem,
    back_sem,
):
    me = lax.axis_index("genes")
    core = lax.axis_index("samples")
    x, y = me // SIDE, me % SIDE
    nxt, prv = (me + 1) % n, (me + n - 1) % n
    other = 1 - core
    xp = jnp.where(y > 0, x, (x + SIDE - 1) % SIDE)

    mine = pltpu.make_async_copy(dose_ref, dose.at[0], local_sem)
    mine.start()
    barrier = pltpu.get_barrier_semaphore()

    @pl.loop(1, n)
    def _(step):
        pl.semaphore_signal(
            barrier, inc=1, device_id={"genes": (me + step) % n}, device_id_type=MESH
        )

    pl.semaphore_signal(barrier, inc=1, device_id={"samples": other}, device_id_type=MESH)

    def send_chunk(dx):
        @pl.loop(0, SIDE)
        def _(yo):
            owner = ((x + dx) % SIDE) * SIDE + yo
            near = (yo - y + SIDE) % SIDE < SIDE // 2
            kind = jnp.where(near, 0, 1)
            dest = jnp.where(near, owner, (owner + 1) % n)

            @pl.when(dest != me)
            def _():
                pltpu.make_async_remote_copy(
                    src_ref=msgs.at[owner],
                    dst_ref=raw.at[kind, me],
                    send_sem=sent_sem.at[0],
                    recv_sem=direct_sem.at[kind, dx],
                    device_id={"genes": dest},
                    device_id_type=MESH,
                ).start()

            @pl.when(dest == me)
            def _():
                pltpu.make_async_copy(
                    msgs.at[owner], raw.at[kind, me], direct_sem.at[kind, dx]
                ).start()

    pl.semaphore_wait(barrier, n)

    @pl.loop(0, SIDE)
    def _(dx):
        send_chunk(dx)

    dose_copy = pltpu.make_async_remote_copy(
        src_ref=dose_ref,
        dst_ref=dose.at[1],
        send_sem=dose_sem.at[0],
        recv_sem=dose_sem.at[1],
        device_id={"samples": other},
        device_id_type=MESH,
    )
    dose_copy.start()
    expr_copy = pltpu.make_async_remote_copy(
        src_ref=expr_ref,
        dst_ref=expr.at[1],
        send_sem=expr_sem.at[0],
        recv_sem=expr_sem.at[1],
        device_id={"genes": nxt},
        device_id_type=MESH,
    )
    expr_copy.start()

    expr[0] = expr_ref[...]
    for kind in range(2):
        total = (keyr_ref[kind] == keyl_ref[kind]).astype(jnp.float32)
        live = (idxr_ref[...] == idxl_ref[kind]).astype(jnp.float32)
        sd[kind, : GENE_DEV * ROWS] = total.astype(jnp.bfloat16)
        sd[kind, GENE_DEV * ROWS :] = live.astype(jnp.bfloat16)
    expr_copy.wait()
    mine.wait()

    ones = jnp.ones((8, ALIGN), jnp.float32)

    def dose_stats(slot, first, rows):
        @pl.loop(0, rows // ALIGN)
        def _(r):
            at = pl.multiple_of(first + r * ALIGN, ALIGN)
            total = jnp.zeros((ALIGN, ALIGN), jnp.float32)
            square = jnp.zeros((ALIGN, ALIGN), jnp.float32)
            for k in range(HALF // ALIGN):
                value = dose[slot, pl.ds(at, ALIGN), k * ALIGN : (k + 1) * ALIGN].astype(jnp.float32)
                total = total + value
                square = square + value * value
            for which, part in enumerate((total, square)):
                stat[slot, which, :, pl.ds(at, ALIGN)] = lax.dot_general(
                    ones,
                    part,
                    NT,
                    precision=lax.Precision.HIGHEST,
                    preferred_element_type=jnp.float32,
                )

    def relay_chunk(dx):
        for kind in range(2):
            pltpu.make_async_copy(
                raw.at[kind, 0 : SIDE // 2], raw.at[kind, 0 : SIDE // 2], direct_sem.at[kind, dx]
            ).wait()
        for kind, partner in ((0, nxt), (1, prv)):
            xs = ((x if kind == 0 else xp) + SIDE - dx) % SIDE

            @pl.loop(0, SIDE // 2)
            def _(t):
                ys = (y + SIDE - t) % SIDE if kind == 0 else (y + t) % SIDE
                source = xs * SIDE + ys
                pltpu.make_async_remote_copy(
                    src_ref=raw.at[kind, source],
                    dst_ref=raw.at[1 - kind, source],
                    send_sem=sent_sem.at[1],
                    recv_sem=relay_sem.at[1 - kind, dx],
                    device_id={"genes": partner},
                    device_id_type=MESH,
                ).start()

    def ratio_chunk(dx):
        for kind in range(2):
            pltpu.make_async_copy(
                raw.at[kind, 0 : SIDE // 2], raw.at[kind, 0 : SIDE // 2], relay_sem.at[kind, dx]
            ).wait()
            xs = ((x if kind == 0 else xp) + SIDE - dx) % SIDE
            counts = raw[kind, pl.ds(xs * SIDE, SIDE)].reshape(ALIGN, LANES)
            both = lax.dot_general(sd[kind], counts, NT, preferred_element_type=jnp.float32)
            total, live = both[: GENE_DEV * ROWS], both[GENE_DEV * ROWS :]
            ratio = live / jnp.maximum(total, 1.0)
            own = expr[kind, :, pl.ds(pl.multiple_of(xs * ALIGN, ALIGN), ALIGN)].astype(jnp.float32)
            row = lax.broadcasted_iota(jnp.int32, (8, ALIGN), 0)
            for g in range(GENE_DEV):
                block = ratio[g * ROWS : (g + 1) * ROWS]
                head = jnp.where(row == 0, own[g : g + 1], block[:8])
                panel[kind, 0, xs, g * ROWS : (g + 1) * ROWS] = jnp.concatenate(
                    [head, block[8:]], axis=0
                ).astype(jnp.bfloat16)

    def panel_copy(kind, dx):
        xs = ((x if kind == 0 else xp) + SIDE - dx) % SIDE
        return pltpu.make_async_remote_copy(
            src_ref=panel.at[kind, 0, xs],
            dst_ref=panel.at[kind, 1, xs],
            send_sem=panel_sem.at[kind, 0],
            recv_sem=panel_sem.at[kind, 1],
            device_id={"samples": other},
            device_id_type=MESH,
        )

    def panel_chunk(dx):
        panel_copy(0, dx).start()

        @pl.when(core == 0)
        def _():
            panel_copy(1, dx).start()

    @pl.loop(0, SIDE // 2)
    def _(dx):
        dose_stats(0, dx * 512, 512)
        relay_chunk(dx)

    dose_copy.wait_recv()

    @pl.loop(0, SIDE // 2)
    def _(dx):
        dose_stats(1, dx * 512, 512)
        relay_chunk(SIDE // 2 + dx)

    ratio_chunk(0)

    @pl.loop(1, SIDE)
    def _(dx):
        ratio_chunk(dx)
        panel_chunk(dx - 1)

    panel_chunk(SIDE - 1)

    count = float(2 * HALF)
    for c in range(W // 512):
        at = slice(c * 512, (c + 1) * 512)
        total = stat[0, 0, :, at] + stat[1, 0, :, at]
        square = stat[0, 1, :, at] + stat[1, 1, :, at]
        stat[0, 0, :, at] = total * (1.0 / count)
        stat[0, 1, :, at] = lax.rsqrt(jnp.maximum(square - total * total / count, 1.0))

    def panel_wait(kind, way):
        pltpu.make_async_copy(panel.at[kind, 1], panel.at[kind, 1], panel_sem.at[kind, way]).wait()

    panel_wait(0, 1)

    @pl.when(core == 1)
    def _():
        panel_wait(1, 1)

    def pheno_stats(kind):
        for g in range(GENE_DEV):
            rows = slice(g * ROWS, (g + 1) * ROWS)
            total = jnp.zeros((ROWS, ALIGN), jnp.float32)
            square = jnp.zeros((ROWS, ALIGN), jnp.float32)
            for slot in range(2):
                for k in range(SIDE):
                    value = panel[kind, slot, k, rows].astype(jnp.float32)
                    total = total + value
                    square = square + value * value
            total = jnp.sum(total, axis=1, keepdims=True)
            square = jnp.sum(square, axis=1, keepdims=True)
            pstat[0, rows] = jnp.broadcast_to(total, (ROWS, ALIGN))
            scale = lax.rsqrt(jnp.maximum(square - total * total / count, 1.0))
            pstat[1, rows] = jnp.broadcast_to(scale, (ROWS, ALIGN))

    STEP = 256

    def assoc(kind, first, out_ref, scale):
        left = [
            jnp.concatenate([panel[kind, slot, k] for k in range(SIDE)], axis=1) for slot in range(2)
        ]

        @pl.loop(0, HALF // STEP)
        def _(c):
            at = pl.multiple_of(first + c * STEP, STEP)
            product = sum(
                lax.dot_general(
                    left[slot], dose[slot, pl.ds(at, STEP)], NT, preferred_element_type=jnp.float32
                )
                for slot in range(2)
            )
            for k in range(STEP // ALIGN):
                here = pl.ds(pl.multiple_of(at + k * ALIGN, ALIGN), ALIGN)
                mean = stat[0, 0, 0:1, here]
                dev = stat[0, 1, 0:1, here] * scale
                part = product[:, k * ALIGN : (k + 1) * ALIGN]
                part = (part - pstat[0] * mean) * dev * pstat[1]
                to = pl.ds(pl.multiple_of(c * STEP + k * ALIGN, ALIGN), ALIGN)
                out_ref[:, to] = part.astype(jnp.bfloat16)

    keep = jnp.where(me == 0, 0.0, 1.0)

    @pl.when(core == 0)
    def _():
        pheno_stats(0)
        assoc(0, 0, z_ref.at[0], 1.0)
        assoc(0, HALF, z_ref.at[1], 1.0)

    @pl.when(core == 1)
    def _():
        give = pltpu.make_async_remote_copy(
            src_ref=back,
            dst_ref=z_ref.at[1],
            send_sem=back_sem.at[0],
            recv_sem=back_sem.at[1],
            device_id={"genes": prv},
            device_id_type=MESH,
        )
        pheno_stats(1)
        assoc(1, 0, back, keep)
        give.start()
        pheno_stats(0)
        assoc(0, HALF, z_ref.at[0], 1.0)
        give.wait()

    dose_copy.wait_send()
    pltpu.make_async_copy(raw.at[0, 0 : n - 2], raw.at[0, 0 : n - 2], sent_sem.at[0]).wait()
    pltpu.make_async_copy(raw.at[0], raw.at[0], sent_sem.at[1]).wait()
    panel_wait(0, 0)

    @pl.when(core == 0)
    def _():
        panel_wait(1, 0)


def cut(start_ref, z_ref, out_ref):
    for g in range(GENE_DEV):
        first = start_ref[g] // ALIGN
        for m in range(HALF // ALIGN):
            t = first + m
            part = z_ref[
                t // SIDE, g * ROWS : (g + 1) * ROWS, pl.ds(pl.multiple_of(t % SIDE * ALIGN, ALIGN), ALIGN)
            ]
            out_ref[g, :, m * ALIGN : (m + 1) * ALIGN] = part[:PHEN]


def keys(sizes, mask):
    until = jnp.arange(8)[:, None] <= jnp.arange(8)[None, :]
    ends = jnp.sum(jnp.where(until, sizes[:, :, None], 0), axis=1)
    slot = jnp.arange(SLOTS, dtype=jnp.int32)
    cluster = jnp.sum((ends[:, None, :] <= slot[None, :, None]).astype(jnp.int32), axis=2)
    gene = jnp.arange(GENE_DEV, dtype=jnp.int32)[:, None]
    key = gene * 16 + cluster
    lane_key = jnp.where(mask > 0, key, -1).reshape(1, GENE_DEV * SLOTS)
    lane_key = jnp.pad(lane_key, ((0, 0), (0, LANES - GENE_DEV * SLOTS)), constant_values=-1)
    lane_idx = jnp.where(mask > 0, gene * SLOTS + slot[None], -1).reshape(1, GENE_DEV * SLOTS)
    lane_idx = jnp.pad(lane_idx, ((0, 0), (0, LANES - GENE_DEV * SLOTS)), constant_values=-1)
    row_key = jnp.pad(key, ((0, 0), (1, ROWS - PHEN)), constant_values=-2)
    return lane_key, lane_idx, row_key.reshape(GENE_DEV * ROWS, 1)


def shards(dosage, expression, intron_counts, cluster_sizes, valid_mask, gene_block, window_start):
    n = lax.axis_size("genes")
    me = lax.axis_index("genes")
    prv = (me + n - 1) % n
    lane_key, lane_idx, row_key = zip(
        *(
            keys(
                lax.dynamic_slice_in_dim(cluster_sizes, i * GENE_DEV, GENE_DEV, 0),
                lax.dynamic_slice_in_dim(valid_mask, i * GENE_DEV, GENE_DEV, 0),
            )
            for i in (me, prv)
        )
    )
    row_idx = jnp.arange(GENE_DEV, dtype=jnp.int32)[:, None] * SLOTS + jnp.arange(SLOTS, dtype=jnp.int32)[None]
    row_idx = jnp.pad(row_idx, ((0, 0), (1, ROWS - PHEN)), constant_values=-2).reshape(GENE_DEV * ROWS, 1)
    vmem = pl.BlockSpec(memory_space=pltpu.VMEM)
    smem = pl.BlockSpec(memory_space=pltpu.SMEM)
    dma = pltpu.SemaphoreType.DMA
    bf16, f32 = jnp.bfloat16, jnp.float32
    rows = GENE_DEV * ROWS
    msgs = pl.pallas_call(
        permute,
        out_shape=jax.ShapeDtypeStruct((n, 16, LANES), bf16),
        in_specs=[smem, vmem],
        out_specs=vmem,
        name="permute",
    )(gene_block, intron_counts)
    z = pl.pallas_call(
        functools.partial(kernel, n),
        out_shape=jax.ShapeDtypeStruct((2, rows, HALF), bf16),
        in_specs=[vmem, vmem, vmem, vmem, vmem, vmem, pl.BlockSpec(memory_space=pl.ANY)],
        out_specs=vmem,
        scratch_shapes=[
            pltpu.VMEM((2, n, 16, LANES), bf16),
            pltpu.VMEM((2, GENE_DEV, HALF), bf16),
            pltpu.VMEM((2, 2, SIDE, rows, ALIGN), bf16),
            pltpu.VMEM((2, W, HALF), bf16),
            pltpu.VMEM((2, 2, 8, W), f32),
            pltpu.VMEM((2, rows, ALIGN), f32),
            pltpu.VMEM((2, 2 * rows, LANES), bf16),
            pltpu.VMEM((rows, HALF), bf16),
            dma((2, SIDE)),
            dma((2, SIDE)),
            dma((2, 2)),
            dma((2,)),
            dma,
            dma((2,)),
            dma((2,)),
            dma((2,)),
        ],
        compiler_params=pltpu.CompilerParams(collective_id=0, has_side_effects=True),
        name="associate",
    )(
        msgs,
        expression,
        jnp.stack(lane_key),
        jnp.stack(lane_idx),
        jnp.stack(row_key),
        row_idx,
        dosage,
    )
    return pl.pallas_call(
        cut,
        out_shape=jax.ShapeDtypeStruct((GENE_DEV, PHEN, HALF), bf16),
        in_specs=[smem, vmem],
        out_specs=vmem,
        name="cut",
    )(window_start, z)


def solution(mesh):
    in_specs = (
        P(("parts", "genes"), "samples"),
        P(("parts", "genes"), "samples"),
        P(("parts", "samples", "genes"), None),
        P("parts", None),
        P("parts", None),
        P("parts"),
        P(("parts", "genes")),
    )
    out_specs = P(("parts", "genes"), None, "samples")
    return jax.shard_map(shards, mesh=mesh, in_specs=in_specs, out_specs=out_specs, check_vma=False)
```

time: 156 us -> 96.4 us (0.62)
  the two profiles are of different devices: /device:TPU:515 before, /device:TPU:513 now
where the time goes in v1:
time: 96.4 us; the launch traced here: 95.8 us
  Pallas kernels  87.6 us (91%)
  local copies, waits for them, and re-layouts  5.81 us (6%)
  other arithmetic  2.31 us (2%)
    pallas_call x1, Pallas kernels, shards(): pl.pallas_call(functools.partial(kernel, n), out_shape=jax.ShapeDtypeStru...  73.2 us
    pallas_call x1, Pallas kernels, shards(): pl.pallas_call(permute, out_shape=jax.ShapeDtypeStruct((n, 16, LANES), bf...  11.6 us
    pallas_call x1, Pallas kernels, shards(): pl.pallas_call(cut, out_shape=jax.ShapeDtypeStruct((GENE_DEV, PHEN, HALF)...  2.79 us
    pallas_call x1, local copies, waits for them, and re-layouts, shards(): pl.pallas_call(cut, out_shape=jax.ShapeDtypeStruct((GENE_DEV, PHEN, HALF)...  2.35 us

profile of v1, /device:TPU:513, one launch (start us, length us, event | category | flops | bytes accessed | tf_op | source)
XLA Modules:
  0.0 95.8 jit_solution(3356016129125407694)
XLA Ops:
  0.0 0.8 constant_dynamic-slice_fusion
  0.8 0.1 copy.44
  0.9 0.1 copy.42
  0.9 0.1 select_reduce_fusion.1
  1.0 0.1 convert_reduce_fusion
  1.1 0.8 constant_dynamic-slice_fusion.3
  2.0 0.1 copy.49
  2.0 0.1 copy.50
  2.1 0.1 fusion.1
  2.2 0.1 reshape.31
  2.3 0.1 reshape.32
  2.4 0.6 pad_add_fusion.2.idxl_ref
  3.0 0.1 pad.29
  3.0 0.1 broadcast_select_fusion.1
  3.1 0.1 reshape.29
  3.2 0.1 reshape.30
  3.3 0.6 pad_add_fusion.1.keyl_ref
  3.9 0.1 pad.27
  4.0 0.1 pad.28
  4.0 0.1 stack_reshape.9
  4.2 0.1 stack_reshape.8
  4.3 0.8 pad_add_fusion.keyr_ref
  5.0 0.8 reshape.34.idxr_ref
  5.8 11.6 %permute.1.msgs = bf16[64,16,384]{2,1,0:T(8,128)(2,1)} custom-call(s32[512]{0:T(512)} %block_ref.1, bf16[16,20480]{1,0:T(8,128)(2,1)} %counts_ref.1), custom_call_target="tpu_custom_call" | custom-call | tf_op jit(solution)/shard_map/permute/pallas_call | solution.py:397
  17.4 73.2 %associate.1.z_ref = bf16[2,384,1024]{2,1,0:T(8,128)(2,1)} custom-call(bf16[64,16,384]{2,1,0:T(8,128)(2,1)} %permute.1.msgs, bf16[8,1024]{1,0:T(8,128)(2,1)} %expr_ref.1, s32[2,1,384]{2,1,0:T(1,128)} %pad_add_fusion.1.keyl_ref, s32[2,1,384]{2,1,0:T(1,128)} %pad_add_fusion.2.idxl_ref, s32[2,384,1]{2,1,0:T(8,128)} %pad_add_fusion.keyr_ref, ...), custom_call_target="tpu_custom_call" | custom-call | tf_op jit(solution)/shard_map/associate/pallas_call | solution.py:404
  90.7 2.8 %cut.1 = bf16[8,41,1024]{2,1,0:T(8,128)(2,1)} custom-call(s32[8]{0:T(128)} %start_ref.1, bf16[2,384,1024]{2,1,0:T(8,128)(2,1)} %associate.1.z_ref), custom_call_target="tpu_custom_call" | custom-call | tf_op jit(solution)/shard_map/cut/pallas_call | solution.py:438
  93.5 2.4 %copy.48 = bf16[8,41,1024]{2,0,1:T(8,128)(2,1)} copy(bf16[8,41,1024]{2,1,0:T(8,128)(2,1)} %cut.1) | data formatting | bytes 1343488 | tf_op jit(solution)/shard_map/cut/pallas_call | solution.py:438
  (6 shorter events, 0.0 us)

commit v2 on v1

v2 whole, which is shorter than its diff:
```python
import functools

import jax
import jax.numpy as jnp
from jax import lax
from jax.experimental import pallas as pl
from jax.experimental.pallas import tpu as pltpu
from jax.sharding import PartitionSpec as P

W = 2048
HALF = 1024
SLOTS = 40
ALIGN = 128
PHEN = 41
ROWS = 336
USED = 328
RATIOS = 320
STEP = 256
GENE_DEV = 8
LANES = 384
SIDE = 8
MESH = pl.DeviceIdType.MESH
NT = (((1,), (1,)), ((), ()))


def mod(value, size):
    return value & (size - 1) if size & (size - 1) == 0 else lax.rem(value, size)


def permuted(counts_ref, block_ref, msgs_ref, owner):
    lane = lax.broadcasted_iota(jnp.int32, (16, ALIGN), 1)
    tiles = [jnp.zeros((16, ALIGN), jnp.float32) for _ in range(3)]
    for j in range(GENE_DEV):
        tile = block_ref[0, owner * GENE_DEV + j]
        start = block_ref[1, owner * GENE_DEV + j]
        a = counts_ref[tile].astype(jnp.float32)
        b = counts_ref[tile + 1].astype(jnp.float32)
        q = j * SLOTS % ALIGN
        turn = q - jnp.broadcast_to(start, (16, ALIGN))
        gene = jnp.where(lane >= start, a, b)
        for bit in (8, 16, 32, 64):
            gene = jnp.where((turn & bit) != 0, pltpu.roll(gene, bit, 1), gene)
        t = j * SLOTS // ALIGN
        tiles[t] = jnp.where((lane >= q) & (lane < q + SLOTS), gene, tiles[t])
        if q + SLOTS > ALIGN:
            tiles[t + 1] = jnp.where(lane < q + SLOTS - ALIGN, gene, tiles[t + 1])
    msgs_ref[owner] = jnp.concatenate(tiles, axis=1).astype(jnp.bfloat16)


def membership(sizes_ref, mask_ref, owner, sd_ref):
    per = ALIGN // GENE_DEV
    at = pl.ds(pl.multiple_of(owner // per * ALIGN, ALIGN), ALIGN)
    turn = (ALIGN - owner % per * GENE_DEV) % ALIGN
    sizes = pltpu.roll(sizes_ref[:, at].astype(jnp.float32), turn, 1)
    mask = pltpu.roll(mask_ref[:, at].astype(jnp.float32), turn, 1)
    slot = lax.broadcasted_iota(jnp.int32, (SLOTS, ALIGN), 0).astype(jnp.float32)
    ends = jnp.zeros((1, ALIGN), jnp.float32)
    cluster = jnp.zeros((SLOTS, ALIGN), jnp.float32)
    for c in range(8):
        ends = ends + sizes[c : c + 1]
        cluster = cluster + (ends <= slot).astype(jnp.float32)

    gene = lax.broadcasted_iota(jnp.int32, (SLOTS, GENE_DEV, ALIGN), 1)
    lane = lax.broadcasted_iota(jnp.int32, (SLOTS, GENE_DEV, ALIGN), 2)
    key = jnp.where(lane == gene, cluster[:, None, :], 0.0)
    key = jnp.sum(key, axis=2, keepdims=True).reshape(RATIOS, 1)
    row = lax.broadcasted_iota(jnp.int32, (RATIOS, 1), 0)
    row_gene = row & (GENE_DEV - 1)
    row_slot = lax.shift_right_logical(row, 3)
    row_key = key + (row_gene * 16).astype(jnp.float32)
    row_spot = row_gene * SLOTS + row_slot

    spot = lax.broadcasted_iota(jnp.int32, (ALIGN, LANES), 1)
    spot_gene = sum((spot >= SLOTS * g).astype(jnp.int32) for g in range(1, GENE_DEV + 1))
    pick = (lax.broadcasted_iota(jnp.int32, (ALIGN, LANES), 0) == spot_gene).astype(jnp.float32)
    spot, spot_gene = spot[:SLOTS], spot_gene[:SLOTS]
    here = lax.broadcasted_iota(jnp.int32, (SLOTS, LANES), 0) == spot - spot_gene * SLOTS

    def laid(value):
        full = lax.dot_general(
            value,
            pick,
            (((1,), (0,)), ((), ())),
            precision=lax.Precision.HIGHEST,
            preferred_element_type=jnp.float32,
        )
        return jnp.sum(jnp.where(here, full, 0.0), axis=0, keepdims=True)

    live = (laid(mask) > 0.5) & (spot[:1] < RATIOS)
    lane_key = jnp.where(live, laid(cluster) + (spot_gene[:1] * 16).astype(jnp.float32), -1.0)
    lane_spot = jnp.where(live, spot[:1], -1)
    sd_ref[:RATIOS] = (row_key == lane_key).astype(jnp.float32).astype(jnp.bfloat16)
    sd_ref[RATIOS:] = (row_spot == lane_spot).astype(jnp.float32).astype(jnp.bfloat16)


def kernel(
    n,
    block_ref,
    counts_hbm,
    expr_ref,
    sizes_ref,
    mask_ref,
    dose_ref,
    z_ref,
    counts_flat,
    counts_ref,
    msgs,
    raw,
    expr,
    panel,
    dose,
    squares,
    stat,
    pstat,
    sd,
    back,
    direct_sem,
    relay_sem,
    panel_sem,
    sent_sem,
    local_sem,
    dose_sem,
    expr_sem,
    back_sem,
    counts_sem,
):
    me = lax.axis_index("genes")
    core = lax.axis_index("samples")
    x, y = lax.shift_right_logical(me, 3), me & (SIDE - 1)
    nxt, prv = mod(me + 1, n), mod(me + n - 1, n)
    other = 1 - core
    xp = jnp.where(y > 0, x, mod(x + SIDE - 1, SIDE))

    load = pltpu.make_async_copy(counts_hbm, counts_flat, counts_sem)
    load.start()
    barrier = pltpu.get_barrier_semaphore()
    pl.semaphore_signal(barrier, inc=1, device_id={"samples": other}, device_id_type=MESH)

    @pl.loop(1, n)
    def _(step):
        pl.semaphore_signal(
            barrier, inc=1, device_id={"genes": mod(me + step, n)}, device_id_type=MESH
        )

    mine = pltpu.make_async_copy(dose_ref, dose.at[0], local_sem)
    mine.start()

    def chunk(i):
        half = lax.shift_right_logical(i + 1, 1)
        return jnp.where((i & 1) == 1, half, mod(SIDE - half, SIDE))

    def send_chunk(dx):
        @pl.loop(0, SIDE)
        def _(yo):
            owner = mod(x + dx, SIDE) * SIDE + yo
            near = mod(yo - y + SIDE, SIDE) < SIDE // 2
            kind = jnp.where(near, 0, 1)
            dest = jnp.where(near, owner, mod(owner + 1, n))

            @pl.when(dest != me)
            def _():
                pltpu.make_async_remote_copy(
                    src_ref=msgs.at[owner],
                    dst_ref=raw.at[kind, me],
                    send_sem=sent_sem.at[0],
                    recv_sem=direct_sem.at[kind, dx],
                    device_id={"genes": dest},
                    device_id_type=MESH,
                ).start()

            @pl.when(dest == me)
            def _():
                pltpu.make_async_copy(
                    msgs.at[owner], raw.at[kind, me], direct_sem.at[kind, dx]
                ).start()

    load.wait()
    with jax.named_scope("permute"):
        for t in range(counts_flat.shape[1] // ALIGN):
            counts_ref[t] = counts_flat[:, t * ALIGN : (t + 1) * ALIGN]
        counts_ref[counts_ref.shape[0] - 1] = counts_flat[:, :ALIGN]

        @pl.loop(0, n)
        def _(owner):
            permuted(counts_ref, block_ref, msgs, owner)

    with jax.named_scope("keys"):
        for kind, owner in enumerate((me, prv)):
            membership(sizes_ref, mask_ref, owner, sd.at[kind])
    expr[0] = expr_ref[...]
    with jax.named_scope("barrier"):
        pl.semaphore_wait(barrier, n)
    expr_copy = pltpu.make_async_remote_copy(
        src_ref=expr_ref,
        dst_ref=expr.at[1],
        send_sem=expr_sem.at[0],
        recv_sem=expr_sem.at[1],
        device_id={"genes": nxt},
        device_id_type=MESH,
    )
    expr_copy.start()
    with jax.named_scope("send"):

        @pl.loop(0, SIDE)
        def _(i):
            send_chunk(chunk(i))

    dose_copy = pltpu.make_async_remote_copy(
        src_ref=dose_ref,
        dst_ref=dose.at[1],
        send_sem=dose_sem.at[0],
        recv_sem=dose_sem.at[1],
        device_id={"samples": other},
        device_id_type=MESH,
    )
    dose_copy.start()
    mine.wait()

    def dose_squares(slot, first, rows):
        for r in range(rows // ALIGN):
            at = pl.ds(pl.multiple_of(first + r * ALIGN, ALIGN), ALIGN)
            square = jnp.zeros((ALIGN, ALIGN), jnp.float32) if slot == 0 else squares[at]
            for k in range(HALF // ALIGN):
                value = dose[slot, at, k * ALIGN : (k + 1) * ALIGN].astype(jnp.float32)
                square = square + value * value
            squares[at] = square

    def relay_chunk(dx):
        for kind in range(2):
            pltpu.make_async_copy(
                raw.at[kind, 0 : SIDE // 2], raw.at[kind, 0 : SIDE // 2], direct_sem.at[kind, dx]
            ).wait()
        for kind, partner in ((0, nxt), (1, prv)):
            xs = mod((x if kind == 0 else xp) + SIDE - dx, SIDE)

            @pl.loop(0, SIDE // 2)
            def _(t):
                ys = mod(y + SIDE - t, SIDE) if kind == 0 else mod(y + t, SIDE)
                source = xs * SIDE + ys
                pltpu.make_async_remote_copy(
                    src_ref=raw.at[kind, source],
                    dst_ref=raw.at[1 - kind, source],
                    send_sem=sent_sem.at[1],
                    recv_sem=relay_sem.at[1 - kind, dx],
                    device_id={"genes": partner},
                    device_id_type=MESH,
                ).start()

    def ratio_chunk(dx):
        for kind in range(2):
            pltpu.make_async_copy(
                raw.at[kind, 0 : SIDE // 2], raw.at[kind, 0 : SIDE // 2], relay_sem.at[kind, dx]
            ).wait()
            xs = mod((x if kind == 0 else xp) + SIDE - dx, SIDE)
            counts = raw[kind, pl.ds(xs * SIDE, SIDE)].reshape(ALIGN, LANES)
            both = lax.dot_general(sd[kind], counts, NT, preferred_element_type=jnp.float32)
            ratio = both[RATIOS:] / jnp.maximum(both[:RATIOS], 1.0)
            own = expr[kind, :, pl.ds(pl.multiple_of(xs * ALIGN, ALIGN), ALIGN)].astype(jnp.float32)
            rest = jnp.ones((ROWS - USED, ALIGN), jnp.float32)
            panel[kind, 0, xs] = jnp.concatenate([own, ratio, rest], axis=0).astype(jnp.bfloat16)

    def panel_copy(kind, dx):
        xs = mod((x if kind == 0 else xp) + SIDE - dx, SIDE)
        return pltpu.make_async_remote_copy(
            src_ref=panel.at[kind, 0, xs],
            dst_ref=panel.at[kind, 1, xs],
            send_sem=panel_sem.at[kind, 0],
            recv_sem=panel_sem.at[kind, 1],
            device_id={"samples": other},
            device_id_type=MESH,
        )

    def panel_chunk(dx):
        panel_copy(0, dx).start()

        @pl.when(core == 0)
        def _():
            panel_copy(1, dx).start()

    def pass_on(i, slot):
        with jax.named_scope("squares"):
            dose_squares(slot, (i & (SIDE // 2 - 1)) * 512, 512)
        with jax.named_scope("relay"):
            relay_chunk(chunk(i))

    pass_on(0, 0)
    pass_on(1, 0)
    expr_copy.wait()

    @pl.loop(2, SIDE // 2)
    def _(i):
        pass_on(i, 0)
        with jax.named_scope("ratio"):
            ratio_chunk(chunk(i - 2))

    with jax.named_scope("dose_wait"):
        dose_copy.wait_recv()

    @pl.loop(SIDE // 2, SIDE)
    def _(i):
        pass_on(i, 1)
        with jax.named_scope("ratio"):
            ratio_chunk(chunk(i - 2))
        panel_chunk(chunk(i - 4))

    count = float(2 * HALF)
    with jax.named_scope("square_rows"):
        for c in range(W // 512):
            at = slice(c * 512, (c + 1) * 512)
            stat[:, at] = lax.dot_general(
                jnp.ones((8, ALIGN), jnp.float32),
                squares[at],
                NT,
                precision=lax.Precision.HIGHEST,
                preferred_element_type=jnp.float32,
            )

    panel_chunk(chunk(SIDE - 4))
    panel_chunk(chunk(SIDE - 3))
    with jax.named_scope("ratio_end"):
        ratio_chunk(chunk(SIDE - 2))
    with jax.named_scope("ratio_end"):
        ratio_chunk(chunk(SIDE - 1))
    panel_chunk(chunk(SIDE - 2))
    panel_chunk(chunk(SIDE - 1))

    def panel_wait(kind, way):
        pltpu.make_async_copy(panel.at[kind, 1], panel.at[kind, 1], panel_sem.at[kind, way]).wait()

    with jax.named_scope("panel_wait"):
        panel_wait(0, 1)

    @pl.when(core == 1)
    def _():
        panel_wait(1, 1)

    def pheno_stats(kind):
        PIECE = 48
        for g in range(ROWS // PIECE):
            rows = slice(g * PIECE, (g + 1) * PIECE)
            total = jnp.zeros((PIECE, ALIGN), jnp.float32)
            square = jnp.zeros((PIECE, ALIGN), jnp.float32)
            for slot in range(2):
                for k in range(SIDE):
                    value = panel[kind, slot, k, rows].astype(jnp.float32)
                    total = total + value
                    square = square + value * value
            total = jnp.sum(total, axis=1, keepdims=True)
            square = jnp.sum(square, axis=1, keepdims=True)
            pstat[0, rows] = jnp.broadcast_to(total, (PIECE, ALIGN))
            scale = lax.rsqrt(jnp.maximum(square - total * total / count, 1.0))
            pstat[1, rows] = jnp.broadcast_to(scale, (PIECE, ALIGN))

    def assoc(kind, first, out_ref, scale, after=None):
        left = [
            jnp.concatenate([panel[kind, slot, k] for k in range(SIDE)], axis=1) for slot in range(2)
        ]

        @pl.loop(0, HALF // STEP)
        def _(c):
            at = pl.multiple_of(first + c * STEP, STEP)
            product = sum(
                lax.dot_general(
                    left[slot], dose[slot, pl.ds(at, STEP)], NT, preferred_element_type=jnp.float32
                )
                for slot in range(2)
            )
            for k in range(STEP // ALIGN):
                here = pl.ds(pl.multiple_of(at + k * ALIGN, ALIGN), ALIGN)
                part = product[:, k * ALIGN : (k + 1) * ALIGN]
                total = part[USED : USED + 1]
                mean = total * (1.0 / count)
                dev = lax.rsqrt(jnp.maximum(stat[0:1, here] - total * mean, 1.0)) * scale
                part = (part - pstat[0] * mean) * dev * pstat[1]
                out_ref[c, :, k * ALIGN : (k + 1) * ALIGN] = part.astype(jnp.bfloat16)
            if after is not None:

                @pl.when(c > 0)
                def _():
                    after(c - 1)

        if after is not None:
            after(HALF // STEP - 1)

    keep = jnp.where(me == 0, 0.0, 1.0)

    def give(c):
        return pltpu.make_async_remote_copy(
            src_ref=back.at[c],
            dst_ref=z_ref.at[1, c],
            send_sem=back_sem.at[0],
            recv_sem=back_sem.at[1],
            device_id={"genes": prv},
            device_id_type=MESH,
        )

    @pl.when(core == 0)
    def _():
        with jax.named_scope("pstats_a"):
            pheno_stats(0)
        with jax.named_scope("assoc_a"):
            assoc(0, 0, z_ref.at[0], 1.0)
            assoc(0, HALF, z_ref.at[1], 1.0)

    @pl.when(core == 1)
    def _():
        with jax.named_scope("pstats_b"):
            pheno_stats(1)
        with jax.named_scope("assoc_b"):
            assoc(1, 0, back, keep, lambda c: give(c).start())
        with jax.named_scope("assoc_c"):
            pheno_stats(0)
            assoc(0, HALF, z_ref.at[0], 1.0)
        with jax.named_scope("back_wait"):
            for way in (1, 0):
                pltpu.make_async_copy(back, back, back_sem.at[way]).wait()

    dose_copy.wait_send()
    pltpu.make_async_copy(raw.at[0, 0 : n - 2], raw.at[0, 0 : n - 2], sent_sem.at[0]).wait()
    pltpu.make_async_copy(raw.at[0], raw.at[0], sent_sem.at[1]).wait()
    panel_wait(0, 0)

    @pl.when(core == 0)
    def _():
        panel_wait(1, 0)


def cut(start_ref, z_ref, out_ref):
    gene = lax.broadcasted_iota(jnp.int32, (ROWS, ALIGN), 0) & (GENE_DEV - 1)

    @pl.loop(0, HALF // ALIGN)
    def _(m):
        part = None
        for g in range(GENE_DEV):
            t = lax.shift_right_logical(start_ref[g], 7) + m
            half = lax.shift_right_logical(t, 3)
            step = lax.shift_right_logical(t, 1) & (HALF // STEP - 1)
            lanes = pl.ds(pl.multiple_of((t & 1) * ALIGN, ALIGN), ALIGN)
            value = z_ref[half, step, :, lanes]
            part = value if g == 0 else jnp.where(gene == g, value, part)
        to = pl.ds(pl.multiple_of(m * ALIGN, ALIGN), ALIGN)
        out_ref[:, :, to] = part[:USED].reshape(PHEN, GENE_DEV, ALIGN)


def shards(dosage, expression, intron_counts, cluster_sizes, valid_mask, gene_block, window_start):
    n = lax.axis_size("genes")
    vmem = pl.BlockSpec(memory_space=pltpu.VMEM)
    smem = pl.BlockSpec(memory_space=pltpu.SMEM)
    hbm = pl.BlockSpec(memory_space=pl.ANY)
    dma = pltpu.SemaphoreType.DMA
    bf16, f32 = jnp.bfloat16, jnp.float32
    z = pl.pallas_call(
        functools.partial(kernel, n),
        out_shape=jax.ShapeDtypeStruct((2, HALF // STEP, ROWS, STEP), bf16),
        in_specs=[smem, hbm, vmem, vmem, vmem, hbm],
        out_specs=vmem,
        scratch_shapes=[
            pltpu.VMEM(intron_counts.shape, bf16),
            pltpu.VMEM((intron_counts.shape[1] // ALIGN + 1, 16, ALIGN), bf16),
            pltpu.VMEM((n, 16, LANES), bf16),
            pltpu.VMEM((2, n, 16, LANES), bf16),
            pltpu.VMEM((2, GENE_DEV, HALF), bf16),
            pltpu.VMEM((2, 2, SIDE, ROWS, ALIGN), bf16),
            pltpu.VMEM((2, W, HALF), bf16),
            pltpu.VMEM((W, ALIGN), f32),
            pltpu.VMEM((8, W), f32),
            pltpu.VMEM((2, ROWS, ALIGN), f32),
            pltpu.VMEM((2, 2 * RATIOS, LANES), bf16),
            pltpu.VMEM((HALF // STEP, ROWS, STEP), bf16),
            dma((2, SIDE)),
            dma((2, SIDE)),
            dma((2, 2)),
            dma((2,)),
            dma,
            dma((2,)),
            dma((2,)),
            dma((2,)),
            dma,
        ],
        compiler_params=pltpu.CompilerParams(collective_id=0, has_side_effects=True),
        name="associate",
    )(
        jnp.stack([gene_block * SLOTS // ALIGN, gene_block * SLOTS % ALIGN]),
        intron_counts,
        expression,
        cluster_sizes.T,
        valid_mask.T,
        dosage,
    )
    out = pl.pallas_call(
        cut,
        out_shape=jax.ShapeDtypeStruct((PHEN, GENE_DEV, HALF), bf16),
        in_specs=[smem, vmem],
        out_specs=vmem,
        name="cut",
    )(window_start, z)
    return jnp.swapaxes(out, 0, 1)


def solution(mesh):
    in_specs = (
        P(("parts", "genes"), "samples"),
        P(("parts", "genes"), "samples"),
        P(("parts", "samples", "genes"), None),
        P("parts", None),
        P("parts", None),
        P("parts"),
        P(("parts", "genes")),
    )
    out_specs = P(("parts", "genes"), None, "samples")
    return jax.shard_map(shards, mesh=mesh, in_specs=in_specs, out_specs=out_specs, check_vma=False)
```

time: 96.4 us -> 89.2 us (0.925)
  local copies, waits for them, and re-layouts: 5.81 us -> 0 us
  other arithmetic: 2.31 us -> 1.29 us
    pallas_call x1, Pallas kernels: 73.2 us -> 84.2 us  [shards(): pl.pallas_call(functools.partial(kernel, n), out_shape=jax.ShapeDtypeStru...]
    pallas_call x2 -> x1, Pallas kernels: 14.4 us -> 3.55 us  [shards(): pl.pallas_call(cut, out_shape=jax.ShapeDtypeStruct((PHEN, GENE_DEV, HALF)...]
    pallas_call x1 -> x0, local copies, waits for them, and re-layouts: 2.35 us -> none  [shards(): pl.pallas_call(cut, out_shape=jax.ShapeDtypeStruct((GENE_DEV, PHEN, HALF)...]
    dynamic_slice x4 -> x0, local copies, waits for them, and re-layouts: 1.75 us -> none  [the longest x3 0.92 us: shards(): lax.dynamic_slice_in_dim(cluster_sizes, i * GENE_DEV, GENE_DEV, 0)]
    another operation x3 -> x1, other arithmetic: 1.96 us -> 0.6 us  [shards(): jnp.stack([gene_block * SLOTS // ALIGN, gene_block * SLOTS % ALIGN])]
    reshape x5 -> x0, local copies, waits for them, and re-layouts: 1.1 us -> none  [the longest x1 0.78 us: shards(): jnp.pad(row_idx, ((0, 0), (1, ROWS - PHEN)), constant_values=-2)]
where the time goes in v2:
time: 89.2 us; the launch traced here: 89 us
  Pallas kernels  87.7 us (98%)
  other arithmetic  1.29 us (1%)
    pallas_call x1, Pallas kernels, shards(): pl.pallas_call(functools.partial(kernel, n), out_shape=jax.ShapeDtypeStru...  84.2 us
    pallas_call x1, Pallas kernels, shards(): pl.pallas_call(cut, out_shape=jax.ShapeDtypeStruct((PHEN, GENE_DEV, HALF)...  3.55 us

profile of v2, /device:TPU:513, one launch (start us, length us, event | category | flops | bytes accessed | tf_op | source)
XLA Modules:
  0.0 89.0 jit_solution(7918785809252090112)
XLA Ops:
  0.0 0.7 add_select_fusion.1
  0.7 0.6 pad_add_fusion.block_ref
  1.3 84.2 %associate.1.z_ref = bf16[2,4,336,256]{3,2,1,0:T(8,128)(2,1)} custom-call(s32[2,512]{1,0:T(2,128)} %pad_add_fusion.block_ref, bf16[16,20480]{1,0:T(8,128)(2,1)} %counts_hbm.1, bf16[8,1024]{1,0:T(8,128)(2,1)} %expr_ref.1, s32[8,512]{1,0:T(8,128)} %bitcast.6, s32[40,512]{1,0:T(8,128)} %bitcast.5, bf16[2048,1024]{1,0:T(8,128)(2,1)} %dose_ref.1), custom_call_target="tpu_custom_call" | custom-call | tf_op jit(solution)/shard_map/associate/pallas_call | solution.py:452
  85.5 3.6 %cut.1 = bf16[41,8,1024]{2,1,0:T(8,128)(2,1)} custom-call(s32[8]{0:T(128)} %start_ref.1, bf16[2,4,336,256]{3,2,1,0:T(8,128)(2,1)} %associate.1.z_ref), custom_call_target="tpu_custom_call" | custom-call | tf_op jit(solution)/shard_map/cut/pallas_call | solution.py:490

commit v3 on v2

--- a/solution.py
+++ b/solution.py
@@ -29,22 +29,21 @@
 
 def permuted(counts_ref, block_ref, msgs_ref, owner):
     lane = lax.broadcasted_iota(jnp.int32, (16, ALIGN), 1)
-    tiles = [jnp.zeros((16, ALIGN), jnp.float32) for _ in range(3)]
+    tiles = [None] * 3
     for j in range(GENE_DEV):
-        tile = block_ref[0, owner * GENE_DEV + j]
-        start = block_ref[1, owner * GENE_DEV + j]
+        first = block_ref[owner * GENE_DEV + j] * SLOTS
+        tile = lax.shift_right_logical(first, 7)
+        start = first & (ALIGN - 1)
         a = counts_ref[tile].astype(jnp.float32)
         b = counts_ref[tile + 1].astype(jnp.float32)
         q = j * SLOTS % ALIGN
-        turn = q - jnp.broadcast_to(start, (16, ALIGN))
-        gene = jnp.where(lane >= start, a, b)
-        for bit in (8, 16, 32, 64):
-            gene = jnp.where((turn & bit) != 0, pltpu.roll(gene, bit, 1), gene)
+        gene = pltpu.roll(jnp.where(lane >= start, a, b), (q - start) & (ALIGN - 1), 1)
         t = j * SLOTS // ALIGN
-        tiles[t] = jnp.where((lane >= q) & (lane < q + SLOTS), gene, tiles[t])
+        tiles[t] = gene if q == 0 else jnp.where(lane >= q, gene, tiles[t])
         if q + SLOTS > ALIGN:
-            tiles[t + 1] = jnp.where(lane < q + SLOTS - ALIGN, gene, tiles[t + 1])
-    msgs_ref[owner] = jnp.concatenate(tiles, axis=1).astype(jnp.bfloat16)
+            tiles[t + 1] = gene
+    packed = jnp.where(lane[:8] < ALIGN // 2, tiles[2][:8], pltpu.roll(tiles[2][8:], ALIGN // 2, 1))
+    msgs_ref[owner] = jnp.concatenate([tiles[0], tiles[1], packed], axis=0).astype(jnp.bfloat16)
 
 
 def membership(sizes_ref, mask_ref, owner, sd_ref):
@@ -95,12 +94,18 @@
 
 def kernel(
     n,
-    block_ref,
+    block_hbm,
+    start_hbm,
     counts_hbm,
     expr_ref,
+    sizes_hbm,
+    mask_hbm,
+    dose_ref,
+    out_ref,
+    block_ref,
+    start_ref,
     sizes_ref,
     mask_ref,
-    dose_ref,
     z_ref,
     counts_flat,
     counts_ref,
@@ -122,7 +127,7 @@
     dose_sem,
     expr_sem,
     back_sem,
-    counts_sem,
+    load_sem,
 ):
     me = lax.axis_index("genes")
     core = lax.axis_index("samples")
@@ -131,8 +136,21 @@
     other = 1 - core
     xp = jnp.where(y > 0, x, mod(x + SIDE - 1, SIDE))
 
-    load = pltpu.make_async_copy(counts_hbm, counts_flat, counts_sem)
-    load.start()
+    loads = [
+        pltpu.make_async_copy(source, to, load_sem.at[k])
+        for k, (source, to) in enumerate(
+            (
+                (counts_hbm, counts_flat),
+                (block_hbm, block_ref),
+                (start_hbm, start_ref),
+                (sizes_hbm, sizes_ref),
+                (mask_hbm, mask_ref),
+                (expr_ref, expr.at[0]),
+            )
+        )
+    ]
+    for load in loads:
+        load.start()
     barrier = pltpu.get_barrier_semaphore()
     pl.semaphore_signal(barrier, inc=1, device_id={"samples": other}, device_id_type=MESH)
 
@@ -174,20 +192,20 @@
                     msgs.at[owner], raw.at[kind, me], direct_sem.at[kind, dx]
                 ).start()
 
-    load.wait()
+    for load in loads:
+        load.wait()
     with jax.named_scope("permute"):
         for t in range(counts_flat.shape[1] // ALIGN):
             counts_ref[t] = counts_flat[:, t * ALIGN : (t + 1) * ALIGN]
         counts_ref[counts_ref.shape[0] - 1] = counts_flat[:, :ALIGN]
 
-        @pl.loop(0, n)
+        @pl.loop(0, n, unroll=8)
         def _(owner):
             permuted(counts_ref, block_ref, msgs, owner)
 
     with jax.named_scope("keys"):
         for kind, owner in enumerate((me, prv)):
             membership(sizes_ref, mask_ref, owner, sd.at[kind])
-    expr[0] = expr_ref[...]
     with jax.named_scope("barrier"):
         pl.semaphore_wait(barrier, n)
     expr_copy = pltpu.make_async_remote_copy(
@@ -252,7 +270,13 @@
                 raw.at[kind, 0 : SIDE // 2], raw.at[kind, 0 : SIDE // 2], relay_sem.at[kind, dx]
             ).wait()
             xs = mod((x if kind == 0 else xp) + SIDE - dx, SIDE)
-            counts = raw[kind, pl.ds(xs * SIDE, SIDE)].reshape(ALIGN, LANES)
+            at = pl.ds(xs * SIDE, SIDE)
+            low = raw[kind, at, :16].reshape(ALIGN, ALIGN)
+            high = raw[kind, at, 16:32].reshape(ALIGN, ALIGN)
+            left = raw[kind, at, 32:].astype(jnp.float32)
+            right = pltpu.roll(left, ALIGN // 2, 2)
+            last = jnp.concatenate([left, right], axis=1).reshape(ALIGN, ALIGN).astype(jnp.bfloat16)
+            counts = jnp.concatenate([low, high, last], axis=1)
             both = lax.dot_general(sd[kind], counts, NT, preferred_element_type=jnp.float32)
             ratio = both[RATIOS:] / jnp.maximum(both[:RATIOS], 1.0)
             own = expr[kind, :, pl.ds(pl.multiple_of(xs * ALIGN, ALIGN), ALIGN)].astype(jnp.float32)
@@ -277,9 +301,10 @@
         def _():
             panel_copy(1, dx).start()
 
-    def pass_on(i, slot):
-        with jax.named_scope("squares"):
-            dose_squares(slot, (i & (SIDE // 2 - 1)) * 512, 512)
+    def pass_on(i, slot=None):
+        if slot is not None:
+            with jax.named_scope("squares"):
+                dose_squares(slot, i * 512, 512)
         with jax.named_scope("relay"):
             relay_chunk(chunk(i))
 
@@ -293,15 +318,20 @@
         with jax.named_scope("ratio"):
             ratio_chunk(chunk(i - 2))
 
-    with jax.named_scope("dose_wait"):
-        dose_copy.wait_recv()
-
     @pl.loop(SIDE // 2, SIDE)
     def _(i):
-        pass_on(i, 1)
+        pass_on(i)
         with jax.named_scope("ratio"):
             ratio_chunk(chunk(i - 2))
         panel_chunk(chunk(i - 4))
+
+    with jax.named_scope("dose_wait"):
+        dose_copy.wait_recv()
+    with jax.named_scope("squares_1"):
+
+        @pl.loop(0, W // 512)
+        def _(i):
+            dose_squares(1, i * 512, 512)
 
     count = float(2 * HALF)
     with jax.named_scope("square_rows"):
@@ -351,7 +381,7 @@
             scale = lax.rsqrt(jnp.maximum(square - total * total / count, 1.0))
             pstat[1, rows] = jnp.broadcast_to(scale, (PIECE, ALIGN))
 
-    def assoc(kind, first, out_ref, scale, after=None):
+    def assoc(kind, first, to_ref, scale, after=None):
         left = [
             jnp.concatenate([panel[kind, slot, k] for k in range(SIDE)], axis=1) for slot in range(2)
         ]
@@ -372,7 +402,7 @@
                 mean = total * (1.0 / count)
                 dev = lax.rsqrt(jnp.maximum(stat[0:1, here] - total * mean, 1.0)) * scale
                 part = (part - pstat[0] * mean) * dev * pstat[1]
-                out_ref[c, :, k * ALIGN : (k + 1) * ALIGN] = part.astype(jnp.bfloat16)
+                to_ref[c * (STEP // ALIGN) + k] = part.astype(jnp.bfloat16)
             if after is not None:
 
                 @pl.when(c > 0)
@@ -384,10 +414,13 @@
 
     keep = jnp.where(me == 0, 0.0, 1.0)
 
+    per = STEP // ALIGN
+    first_half, second_half = z_ref.at[0:SIDE], z_ref.at[SIDE : 2 * SIDE]
+
     def give(c):
         return pltpu.make_async_remote_copy(
-            src_ref=back.at[c],
-            dst_ref=z_ref.at[1, c],
+            src_ref=back.at[pl.ds(c * per, per)],
+            dst_ref=z_ref.at[pl.ds(SIDE + c * per, per)],
             send_sem=back_sem.at[0],
             recv_sem=back_sem.at[1],
             device_id={"genes": prv},
@@ -399,8 +432,8 @@
         with jax.named_scope("pstats_a"):
             pheno_stats(0)
         with jax.named_scope("assoc_a"):
-            assoc(0, 0, z_ref.at[0], 1.0)
-            assoc(0, HALF, z_ref.at[1], 1.0)
+            assoc(0, 0, first_half, 1.0)
+            assoc(0, HALF, second_half, 1.0)
 
     @pl.when(core == 1)
     def _():
@@ -410,10 +443,22 @@
             assoc(1, 0, back, keep, lambda c: give(c).start())
         with jax.named_scope("assoc_c"):
             pheno_stats(0)
-            assoc(0, HALF, z_ref.at[0], 1.0)
+            assoc(0, HALF, first_half, 1.0)
         with jax.named_scope("back_wait"):
             for way in (1, 0):
                 pltpu.make_async_copy(back, back, back_sem.at[way]).wait()
+
+    with jax.named_scope("cut"):
+        gene = lax.broadcasted_iota(jnp.int32, (ROWS, ALIGN), 0) & (GENE_DEV - 1)
+
+        @pl.loop(0, HALF // ALIGN)
+        def _(m):
+            part = None
+            for g in range(GENE_DEV):
+                value = z_ref[lax.shift_right_logical(start_ref[g], 7) + m]
+                part = value if g == 0 else jnp.where(gene == g, value, part)
+            to = pl.ds(pl.multiple_of(m * ALIGN, ALIGN), ALIGN)
+            out_ref[:, :, to] = part[:USED].reshape(PHEN, GENE_DEV, ALIGN)
 
     dose_copy.wait_send()
     pltpu.make_async_copy(raw.at[0, 0 : n - 2], raw.at[0, 0 : n - 2], sent_sem.at[0]).wait()
@@ -425,40 +470,25 @@
         panel_wait(1, 0)
 
 
-def cut(start_ref, z_ref, out_ref):
-    gene = lax.broadcasted_iota(jnp.int32, (ROWS, ALIGN), 0) & (GENE_DEV - 1)
-
-    @pl.loop(0, HALF // ALIGN)
-    def _(m):
-        part = None
-        for g in range(GENE_DEV):
-            t = lax.shift_right_logical(start_ref[g], 7) + m
-            half = lax.shift_right_logical(t, 3)
-            step = lax.shift_right_logical(t, 1) & (HALF // STEP - 1)
-            lanes = pl.ds(pl.multiple_of((t & 1) * ALIGN, ALIGN), ALIGN)
-            value = z_ref[half, step, :, lanes]
-            part = value if g == 0 else jnp.where(gene == g, value, part)
-        to = pl.ds(pl.multiple_of(m * ALIGN, ALIGN), ALIGN)
-        out_ref[:, :, to] = part[:USED].reshape(PHEN, GENE_DEV, ALIGN)
-
-
 def shards(dosage, expression, intron_counts, cluster_sizes, valid_mask, gene_block, window_start):
     n = lax.axis_size("genes")
-    vmem = pl.BlockSpec(memory_space=pltpu.VMEM)
-    smem = pl.BlockSpec(memory_space=pltpu.SMEM)
-    hbm = pl.BlockSpec(memory_space=pl.ANY)
     dma = pltpu.SemaphoreType.DMA
     bf16, f32 = jnp.bfloat16, jnp.float32
-    z = pl.pallas_call(
+    out = pl.pallas_call(
         functools.partial(kernel, n),
-        out_shape=jax.ShapeDtypeStruct((2, HALF // STEP, ROWS, STEP), bf16),
-        in_specs=[smem, hbm, vmem, vmem, vmem, hbm],
-        out_specs=vmem,
+        out_shape=jax.ShapeDtypeStruct((PHEN, GENE_DEV, HALF), bf16),
+        in_specs=[pl.BlockSpec(memory_space=pl.ANY)] * 7,
+        out_specs=pl.BlockSpec(memory_space=pltpu.VMEM),
         scratch_shapes=[
+            pltpu.SMEM(gene_block.shape, jnp.int32),
+            pltpu.SMEM(window_start.shape, jnp.int32),
+            pltpu.VMEM(cluster_sizes.shape[::-1], jnp.int32),
+            pltpu.VMEM(valid_mask.shape[::-1], jnp.int32),
+            pltpu.VMEM((2 * SIDE, ROWS, ALIGN), bf16),
             pltpu.VMEM(intron_counts.shape, bf16),
             pltpu.VMEM((intron_counts.shape[1] // ALIGN + 1, 16, ALIGN), bf16),
-            pltpu.VMEM((n, 16, LANES), bf16),
-            pltpu.VMEM((2, n, 16, LANES), bf16),
+            pltpu.VMEM((n, SLOTS, ALIGN), bf16),
+            pltpu.VMEM((2, n, SLOTS, ALIGN), bf16),
             pltpu.VMEM((2, GENE_DEV, HALF), bf16),
             pltpu.VMEM((2, 2, SIDE, ROWS, ALIGN), bf16),
             pltpu.VMEM((2, W, HALF), bf16),
@@ -466,7 +496,7 @@
             pltpu.VMEM((8, W), f32),
             pltpu.VMEM((2, ROWS, ALIGN), f32),
             pltpu.VMEM((2, 2 * RATIOS, LANES), bf16),
-            pltpu.VMEM((HALF // STEP, ROWS, STEP), bf16),
+            pltpu.VMEM((SIDE, ROWS, ALIGN), bf16),
             dma((2, SIDE)),
             dma((2, SIDE)),
             dma((2, 2)),
@@ -475,25 +505,19 @@
             dma((2,)),
             dma((2,)),
             dma((2,)),
-            dma,
+            dma((6,)),
         ],
         compiler_params=pltpu.CompilerParams(collective_id=0, has_side_effects=True),
         name="associate",
     )(
-        jnp.stack([gene_block * SLOTS // ALIGN, gene_block * SLOTS % ALIGN]),
+        gene_block,
+        window_start,
         intron_counts,
         expression,
         cluster_sizes.T,
         valid_mask.T,
         dosage,
     )
-    out = pl.pallas_call(
-        cut,
-        out_shape=jax.ShapeDtypeStruct((PHEN, GENE_DEV, HALF), bf16),
-        in_specs=[smem, vmem],
-        out_specs=vmem,
-        name="cut",
-    )(window_start, z)
     return jnp.swapaxes(out, 0, 1)
 
 

time: 89.2 us -> 67.7 us (0.76)
  Pallas kernels: 87.7 us -> 65.6 us
  local copies, waits for them, and re-layouts: 0 us -> 1.98 us
  other arithmetic: 1.29 us -> 0 us
    pallas_call x1, Pallas kernels: 84.2 us -> 65.6 us  [shards(): pl.pallas_call(functools.partial(kernel, n), out_shape=jax.ShapeDtypeStru...]
    pallas_call x1 -> x0, Pallas kernels: 3.55 us -> none  [shards(): pl.pallas_call(cut, out_shape=jax.ShapeDtypeStruct((PHEN, GENE_DEV, HALF)...]
    unnamed x0 -> x1, local copies, waits for them, and re-layouts: none -> 1.98 us
where the time goes in v3:
time: 67.7 us; the launch traced here: 67.6 us
  Pallas kernels  65.6 us (97%)
  local copies, waits for them, and re-layouts  1.98 us (3%)
    pallas_call x1, Pallas kernels, shards(): pl.pallas_call(functools.partial(kernel, n), out_shape=jax.ShapeDtypeStru...  65.6 us
    unnamed x1, local copies, waits for them, and re-layouts  1.98 us

profile of v3, /device:TPU:513, one launch (start us, length us, event | category | flops | bytes accessed | tf_op | source)
XLA Modules:
  0.0 67.6 jit_solution(9091327944233733304)
XLA Ops:
  0.0 65.6 %associate.1 = bf16[41,8,1024]{2,1,0:T(8,128)(2,1)} custom-call(s32[512]{0:T(512)} %block_hbm.1, s32[8]{0:T(128)} %start_hbm.1, bf16[16,20480]{1,0:T(8,128)(2,1)} %counts_hbm.1, bf16[8,1024]{1,0:T(8,128)(2,1)} %expr_ref.1, s32[8,512]{1,0:T(8,128)} %bitcast.5, s32[40,512]{1,0:T(8,128)} %bitcast.4, bf16[2048,1024]{1,0:T(8,128)(2,1)} %dose_ref.1), custom_call_target="tpu_custom_call" | custom-call | tf_op jit(solution)/shard_map/associate/pallas_call | solution.py:477
  65.6 2.0 %copy.9 = bf16[8,41,1024]{2,0,1:T(8,128)(2,1)} copy(bf16[8,41,1024]{2,0,1:T(8,128)(2,1)} %bitcast.3) | data formatting | bytes 1343488

commit v4 on v3

--- a/solution.py
+++ b/solution.py
@@ -119,6 +119,9 @@
     pstat,
     sd,
     back,
+    land,
+    partial,
+    result,
     direct_sem,
     relay_sem,
     panel_sem,
@@ -127,6 +130,8 @@
     dose_sem,
     expr_sem,
     back_sem,
+    back_send_sem,
+    out_sem,
     load_sem,
 ):
     me = lax.axis_index("genes")
@@ -168,7 +173,7 @@
         return jnp.where((i & 1) == 1, half, mod(SIDE - half, SIDE))
 
     def send_chunk(dx):
-        @pl.loop(0, SIDE)
+        @pl.loop(0, SIDE, unroll=4)
         def _(yo):
             owner = mod(x + dx, SIDE) * SIDE + yo
             near = mod(yo - y + SIDE, SIDE) < SIDE // 2
@@ -203,9 +208,6 @@
         def _(owner):
             permuted(counts_ref, block_ref, msgs, owner)
 
-    with jax.named_scope("keys"):
-        for kind, owner in enumerate((me, prv)):
-            membership(sizes_ref, mask_ref, owner, sd.at[kind])
     with jax.named_scope("barrier"):
         pl.semaphore_wait(barrier, n)
     expr_copy = pltpu.make_async_remote_copy(
@@ -232,6 +234,9 @@
         device_id_type=MESH,
     )
     dose_copy.start()
+    with jax.named_scope("keys"):
+        for kind, owner in enumerate((me, prv)):
+            membership(sizes_ref, mask_ref, owner, sd.at[kind])
     mine.wait()
 
     def dose_squares(slot, first, rows):
@@ -308,22 +313,13 @@
         with jax.named_scope("relay"):
             relay_chunk(chunk(i))
 
-    pass_on(0, 0)
-    pass_on(1, 0)
-    expr_copy.wait()
-
-    @pl.loop(2, SIDE // 2)
+    @pl.loop(0, SIDE // 2)
     def _(i):
         pass_on(i, 0)
-        with jax.named_scope("ratio"):
-            ratio_chunk(chunk(i - 2))
 
     @pl.loop(SIDE // 2, SIDE)
     def _(i):
         pass_on(i)
-        with jax.named_scope("ratio"):
-            ratio_chunk(chunk(i - 2))
-        panel_chunk(chunk(i - 4))
 
     with jax.named_scope("dose_wait"):
         dose_copy.wait_recv()
@@ -345,14 +341,29 @@
                 preferred_element_type=jnp.float32,
             )
 
-    panel_chunk(chunk(SIDE - 4))
-    panel_chunk(chunk(SIDE - 3))
-    with jax.named_scope("ratio_end"):
-        ratio_chunk(chunk(SIDE - 2))
-    with jax.named_scope("ratio_end"):
-        ratio_chunk(chunk(SIDE - 1))
-    panel_chunk(chunk(SIDE - 2))
+    expr_copy.wait()
+    with jax.named_scope("ratio"):
+        ratio_chunk(chunk(0))
+
+    @pl.loop(1, SIDE)
+    def _(i):
+        with jax.named_scope("ratio"):
+            ratio_chunk(chunk(i))
+        panel_chunk(chunk(i - 1))
+
+    def joined(kind, slot):
+        return jnp.concatenate([panel[kind, slot, k] for k in range(SIDE)], axis=1)
+
+    first_left = joined(core, 0)
     panel_chunk(chunk(SIDE - 1))
+    with jax.named_scope("partial"):
+
+        @pl.loop(0, HALF // STEP)
+        def _(c):
+            at = pl.multiple_of(c * STEP, STEP)
+            partial[c] = lax.dot_general(
+                first_left, dose[0, pl.ds(at, STEP)], NT, preferred_element_type=jnp.float32
+            )
 
     def panel_wait(kind, way):
         pltpu.make_async_copy(panel.at[kind, 1], panel.at[kind, 1], panel_sem.at[kind, way]).wait()
@@ -382,19 +393,27 @@
             pstat[1, rows] = jnp.broadcast_to(scale, (PIECE, ALIGN))
 
     def assoc(kind, first, to_ref, scale, after=None):
-        left = [
-            jnp.concatenate([panel[kind, slot, k] for k in range(SIDE)], axis=1) for slot in range(2)
-        ]
+        left = joined(kind, 1)
+        base = None if first == 0 else joined(kind, 0)
 
         @pl.loop(0, HALF // STEP)
         def _(c):
             at = pl.multiple_of(first + c * STEP, STEP)
-            product = sum(
-                lax.dot_general(
-                    left[slot], dose[slot, pl.ds(at, STEP)], NT, preferred_element_type=jnp.float32
+            product = lax.dot_general(
+                left, dose[1, pl.ds(at, STEP)], NT, preferred_element_type=jnp.float32
+            )
+            if base is None:
+                product = product + partial[c]
+            else:
+                product = product + lax.dot_general(
+                    base, dose[0, pl.ds(at, STEP)], NT, preferred_element_type=jnp.float32
                 )
-                for slot in range(2)
-            )
+            if after is not None:
+
+                @pl.when(c > 0)
+                def _():
+                    after(c - 1)
+
             for k in range(STEP // ALIGN):
                 here = pl.ds(pl.multiple_of(at + k * ALIGN, ALIGN), ALIGN)
                 part = product[:, k * ALIGN : (k + 1) * ALIGN]
@@ -403,12 +422,6 @@
                 dev = lax.rsqrt(jnp.maximum(stat[0:1, here] - total * mean, 1.0)) * scale
                 part = (part - pstat[0] * mean) * dev * pstat[1]
                 to_ref[c * (STEP // ALIGN) + k] = part.astype(jnp.bfloat16)
-            if after is not None:
-
-                @pl.when(c > 0)
-                def _():
-                    after(c - 1)
-
         if after is not None:
             after(HALF // STEP - 1)
 
@@ -420,9 +433,9 @@
     def give(c):
         return pltpu.make_async_remote_copy(
             src_ref=back.at[pl.ds(c * per, per)],
-            dst_ref=z_ref.at[pl.ds(SIDE + c * per, per)],
-            send_sem=back_sem.at[0],
-            recv_sem=back_sem.at[1],
+            dst_ref=land.at[pl.ds(c * per, per)],
+            send_sem=back_send_sem,
+            recv_sem=back_sem.at[c],
             device_id={"genes": prv},
             device_id_type=MESH,
         )
@@ -444,21 +457,44 @@
         with jax.named_scope("assoc_c"):
             pheno_stats(0)
             assoc(0, HALF, first_half, 1.0)
-        with jax.named_scope("back_wait"):
-            for way in (1, 0):
-                pltpu.make_async_copy(back, back, back_sem.at[way]).wait()
+
+    gene = lax.broadcasted_iota(jnp.int32, (ROWS, ALIGN), 0) & (GENE_DEV - 1)
+
+    def write(c):
+        to = pl.ds(pl.multiple_of(c * STEP, STEP), STEP)
+        return pltpu.make_async_copy(result.at[c], out_ref.at[:, :, to], out_sem.at[c])
 
     with jax.named_scope("cut"):
-        gene = lax.broadcasted_iota(jnp.int32, (ROWS, ALIGN), 0) & (GENE_DEV - 1)
-
-        @pl.loop(0, HALF // ALIGN)
-        def _(m):
-            part = None
-            for g in range(GENE_DEV):
-                value = z_ref[lax.shift_right_logical(start_ref[g], 7) + m]
-                part = value if g == 0 else jnp.where(gene == g, value, part)
-            to = pl.ds(pl.multiple_of(m * ALIGN, ALIGN), ALIGN)
-            out_ref[:, :, to] = part[:USED].reshape(PHEN, GENE_DEV, ALIGN)
+
+        @pl.loop(0, HALF // STEP)
+        def _(c):
+            @pl.when(core == 1)
+            def _():
+                piece = land.at[pl.ds(c * per, per)]
+                pltpu.make_async_copy(piece, piece, back_sem.at[c]).wait()
+                for k in range(per):
+                    z_ref[SIDE + c * per + k] = land[c * per + k]
+
+            for k in range(per):
+                part = None
+                for g in range(GENE_DEV):
+                    value = z_ref[lax.shift_right_logical(start_ref[g], 7) + (c * per + k)]
+                    part = value if g == 0 else jnp.where(gene == g, value, part)
+                result[c, :, :, k * ALIGN : (k + 1) * ALIGN] = part[:USED].reshape(
+                    PHEN, GENE_DEV, ALIGN
+                )
+
+            @pl.when(c > 0)
+            def _():
+                write(c - 1).start()
+
+        write(HALF // STEP - 1).start()
+        for c in range(HALF // STEP):
+            write(c).wait()
+
+    @pl.when(core == 1)
+    def _():
+        pltpu.make_async_copy(back, back, back_send_sem).wait()
 
     dose_copy.wait_send()
     pltpu.make_async_copy(raw.at[0, 0 : n - 2], raw.at[0, 0 : n - 2], sent_sem.at[0]).wait()
@@ -478,7 +514,7 @@
         functools.partial(kernel, n),
         out_shape=jax.ShapeDtypeStruct((PHEN, GENE_DEV, HALF), bf16),
         in_specs=[pl.BlockSpec(memory_space=pl.ANY)] * 7,
-        out_specs=pl.BlockSpec(memory_space=pltpu.VMEM),
+        out_specs=pl.BlockSpec(memory_space=pl.ANY),
         scratch_shapes=[
             pltpu.SMEM(gene_block.shape, jnp.int32),
             pltpu.SMEM(window_start.shape, jnp.int32),
@@ -497,6 +533,9 @@
             pltpu.VMEM((2, ROWS, ALIGN), f32),
             pltpu.VMEM((2, 2 * RATIOS, LANES), bf16),
             pltpu.VMEM((SIDE, ROWS, ALIGN), bf16),
+            pltpu.VMEM((SIDE, ROWS, ALIGN), bf16),
+            pltpu.VMEM((HALF // STEP, ROWS, STEP), f32),
+            pltpu.VMEM((HALF // STEP, PHEN, GENE_DEV, STEP), bf16),
             dma((2, SIDE)),
             dma((2, SIDE)),
             dma((2, 2)),
@@ -504,7 +543,9 @@
             dma,
             dma((2,)),
             dma((2,)),
-            dma((2,)),
+            dma((HALF // STEP,)),
+            dma,
+            dma((HALF // STEP,)),
             dma((6,)),
         ],
         compiler_params=pltpu.CompilerParams(collective_id=0, has_side_effects=True),

time: 67.7 us -> 62.4 us (0.922)
  Pallas kernels: 65.6 us -> 60.2 us
    pallas_call x1, Pallas kernels: 65.6 us -> 60.2 us  [shards(): pl.pallas_call(functools.partial(kernel, n), out_shape=jax.ShapeDtypeStru...]
where the time goes in v4:
time: 62.4 us; the launch traced here: 62.2 us
  Pallas kernels  60.2 us (96%)
  local copies, waits for them, and re-layouts  1.98 us (3%)
    pallas_call x1, Pallas kernels, shards(): pl.pallas_call(functools.partial(kernel, n), out_shape=jax.ShapeDtypeStru...  60.2 us
    unnamed x1, local copies, waits for them, and re-layouts  1.98 us

profile of v4, /device:TPU:513, one launch (start us, length us, event | category | flops | bytes accessed | tf_op | source)
XLA Modules:
  0.0 62.2 jit_solution(11079013081509140663)
XLA Ops:
  0.0 60.2 %associate.1 = bf16[41,8,1024]{2,1,0:T(8,128)(2,1)} custom-call(s32[512]{0:T(512)} %block_hbm.1, s32[8]{0:T(128)} %start_hbm.1, bf16[16,20480]{1,0:T(8,128)(2,1)} %counts_hbm.1, bf16[8,1024]{1,0:T(8,128)(2,1)} %expr_ref.1, s32[8,512]{1,0:T(8,128)} %bitcast.5, s32[40,512]{1,0:T(8,128)} %bitcast.4, bf16[2048,1024]{1,0:T(8,128)(2,1)} %dose_ref.1), custom_call_target="tpu_custom_call" | custom-call | tf_op jit(solution)/shard_map/associate/pallas_call | solution.py:513
  60.2 2.0 %copy.9 = bf16[8,41,1024]{2,0,1:T(8,128)(2,1)} copy(bf16[8,41,1024]{2,0,1:T(8,128)(2,1)} %bitcast.3) | data formatting | bytes 1343488

commit v5 on v4

--- a/solution.py
+++ b/solution.py
@@ -248,13 +248,16 @@
                 square = square + value * value
             squares[at] = square
 
+    def column(kind, dx):
+        return mod((x if kind == 0 else xp) + SIDE - dx, SIDE)
+
     def relay_chunk(dx):
         for kind in range(2):
             pltpu.make_async_copy(
                 raw.at[kind, 0 : SIDE // 2], raw.at[kind, 0 : SIDE // 2], direct_sem.at[kind, dx]
             ).wait()
         for kind, partner in ((0, nxt), (1, prv)):
-            xs = mod((x if kind == 0 else xp) + SIDE - dx, SIDE)
+            xs = column(kind, dx)
 
             @pl.loop(0, SIDE // 2)
             def _(t):
@@ -269,27 +272,34 @@
                     device_id_type=MESH,
                 ).start()
 
-    def ratio_chunk(dx):
+    def slots_of(kind, xs):
+        at = pl.ds(xs * SIDE, SIDE)
+        low = raw[kind, at, :16].reshape(ALIGN, ALIGN)
+        high = raw[kind, at, 16:32].reshape(ALIGN, ALIGN)
+        left = raw[kind, at, 32:].astype(jnp.float32)
+        right = pltpu.roll(left, ALIGN // 2, 2)
+        last = jnp.concatenate([left, right], axis=1).reshape(ALIGN, ALIGN).astype(jnp.bfloat16)
+        return jnp.concatenate([low, high, last], axis=1)
+
+    def ratio_pair(p):
+        pair = (chunk(2 * p), chunk(2 * p + 1))
+        for dx in pair:
+            for kind in range(2):
+                part = raw.at[kind, 0 : SIDE // 2]
+                pltpu.make_async_copy(part, part, relay_sem.at[kind, dx]).wait()
         for kind in range(2):
-            pltpu.make_async_copy(
-                raw.at[kind, 0 : SIDE // 2], raw.at[kind, 0 : SIDE // 2], relay_sem.at[kind, dx]
-            ).wait()
-            xs = mod((x if kind == 0 else xp) + SIDE - dx, SIDE)
-            at = pl.ds(xs * SIDE, SIDE)
-            low = raw[kind, at, :16].reshape(ALIGN, ALIGN)
-            high = raw[kind, at, 16:32].reshape(ALIGN, ALIGN)
-            left = raw[kind, at, 32:].astype(jnp.float32)
-            right = pltpu.roll(left, ALIGN // 2, 2)
-            last = jnp.concatenate([left, right], axis=1).reshape(ALIGN, ALIGN).astype(jnp.bfloat16)
-            counts = jnp.concatenate([low, high, last], axis=1)
+            columns = [column(kind, dx) for dx in pair]
+            counts = jnp.concatenate([slots_of(kind, xs) for xs in columns], axis=0)
             both = lax.dot_general(sd[kind], counts, NT, preferred_element_type=jnp.float32)
             ratio = both[RATIOS:] / jnp.maximum(both[:RATIOS], 1.0)
-            own = expr[kind, :, pl.ds(pl.multiple_of(xs * ALIGN, ALIGN), ALIGN)].astype(jnp.float32)
             rest = jnp.ones((ROWS - USED, ALIGN), jnp.float32)
-            panel[kind, 0, xs] = jnp.concatenate([own, ratio, rest], axis=0).astype(jnp.bfloat16)
+            for k, xs in enumerate(columns):
+                own = expr[kind, :, pl.ds(pl.multiple_of(xs * ALIGN, ALIGN), ALIGN)].astype(jnp.float32)
+                part = ratio[:, k * ALIGN : (k + 1) * ALIGN]
+                panel[kind, 0, xs] = jnp.concatenate([own, part, rest], axis=0).astype(jnp.bfloat16)
 
     def panel_copy(kind, dx):
-        xs = mod((x if kind == 0 else xp) + SIDE - dx, SIDE)
+        xs = column(kind, dx)
         return pltpu.make_async_remote_copy(
             src_ref=panel.at[kind, 0, xs],
             dst_ref=panel.at[kind, 1, xs],
@@ -317,9 +327,40 @@
     def _(i):
         pass_on(i, 0)
 
-    @pl.loop(SIDE // 2, SIDE)
-    def _(i):
-        pass_on(i)
+    expr_copy.wait()
+
+    def pair_out(p):
+        panel_chunk(chunk(2 * p))
+        panel_chunk(chunk(2 * p + 1))
+
+    @pl.loop(2, SIDE // 2)
+    def _(p):
+        pass_on(2 * p)
+        pass_on(2 * p + 1)
+        with jax.named_scope("ratio"):
+            ratio_pair(p - 2)
+
+    pair_out(0)
+    pair_out(1)
+    for p in (2, 3):
+        with jax.named_scope("ratio_end"):
+            ratio_pair(p)
+        if p > 2:
+            pair_out(p - 1)
+
+    def joined(kind, slot):
+        return jnp.concatenate([panel[kind, slot, k] for k in range(SIDE)], axis=1)
+
+    first_left = joined(core, 0)
+    pair_out(SIDE // 2 - 1)
+    with jax.named_scope("partial"):
+
+        @pl.loop(0, HALF // STEP)
+        def _(c):
+            at = pl.multiple_of(c * STEP, STEP)
+            partial[c] = lax.dot_general(
+                first_left, dose[0, pl.ds(at, STEP)], NT, preferred_element_type=jnp.float32
+            )
 
     with jax.named_scope("dose_wait"):
         dose_copy.wait_recv()
@@ -339,30 +380,6 @@
                 NT,
                 precision=lax.Precision.HIGHEST,
                 preferred_element_type=jnp.float32,
-            )
-
-    expr_copy.wait()
-    with jax.named_scope("ratio"):
-        ratio_chunk(chunk(0))
-
-    @pl.loop(1, SIDE)
-    def _(i):
-        with jax.named_scope("ratio"):
-            ratio_chunk(chunk(i))
-        panel_chunk(chunk(i - 1))
-
-    def joined(kind, slot):
-        return jnp.concatenate([panel[kind, slot, k] for k in range(SIDE)], axis=1)
-
-    first_left = joined(core, 0)
-    panel_chunk(chunk(SIDE - 1))
-    with jax.named_scope("partial"):
-
-        @pl.loop(0, HALF // STEP)
-        def _(c):
-            at = pl.multiple_of(c * STEP, STEP)
-            partial[c] = lax.dot_general(
-                first_left, dose[0, pl.ds(at, STEP)], NT, preferred_element_type=jnp.float32
             )
 
     def panel_wait(kind, way):

time: 62.4 us -> 61.3 us (0.982)
  Pallas kernels: 60.2 us -> 59.2 us
    pallas_call x1, Pallas kernels: 60.2 us -> 59.2 us  [shards(): pl.pallas_call(functools.partial(kernel, n), out_shape=jax.ShapeDtypeStru...]
where the time goes in v5:
time: 61.3 us; the launch traced here: 61.2 us
  Pallas kernels  59.2 us (97%)
  local copies, waits for them, and re-layouts  1.98 us (3%)
    pallas_call x1, Pallas kernels, shards(): pl.pallas_call(functools.partial(kernel, n), out_shape=jax.ShapeDtypeStru...  59.2 us
    unnamed x1, local copies, waits for them, and re-layouts  1.98 us

profile of v5, /device:TPU:513, one launch (start us, length us, event | category | flops | bytes accessed | tf_op | source)
XLA Modules:
  0.0 61.2 jit_solution(3185727702558703422)
XLA Ops:
  0.0 59.2 %associate.1 = bf16[41,8,1024]{2,1,0:T(8,128)(2,1)} custom-call(s32[512]{0:T(512)} %block_hbm.1, s32[8]{0:T(128)} %start_hbm.1, bf16[16,20480]{1,0:T(8,128)(2,1)} %counts_hbm.1, bf16[8,1024]{1,0:T(8,128)(2,1)} %expr_ref.1, s32[8,512]{1,0:T(8,128)} %bitcast.5, s32[40,512]{1,0:T(8,128)} %bitcast.4, bf16[2048,1024]{1,0:T(8,128)(2,1)} %dose_ref.1), custom_call_target="tpu_custom_call" | custom-call | tf_op jit(solution)/shard_map/associate/pallas_call | solution.py:530
  59.2 2.0 %copy.9 = bf16[8,41,1024]{2,0,1:T(8,128)(2,1)} copy(bf16[8,41,1024]{2,0,1:T(8,128)(2,1)} %bitcast.3) | data formatting | bytes 1343488

commit v6 on v5

--- a/solution.py
+++ b/solution.py
@@ -139,6 +139,7 @@
     x, y = lax.shift_right_logical(me, 3), me & (SIDE - 1)
     nxt, prv = mod(me + 1, n), mod(me + n - 1, n)
     other = 1 - core
+    inside = (y == 1) | (y == SIDE - 2)
     xp = jnp.where(y > 0, x, mod(x + SIDE - 1, SIDE))
 
     loads = [
@@ -197,6 +198,17 @@
                     msgs.at[owner], raw.at[kind, me], direct_sem.at[kind, dx]
                 ).start()
 
+            @pl.when((yo == SIDE - 1) & inside)
+            def _():
+                pltpu.make_async_remote_copy(
+                    src_ref=msgs.at[owner],
+                    dst_ref=raw.at[1 - kind, me],
+                    send_sem=sent_sem.at[2],
+                    recv_sem=relay_sem.at[1 - kind, dx],
+                    device_id={"genes": jnp.where(near, mod(owner + 1, n), owner)},
+                    device_id_type=MESH,
+                ).start()
+
     for load in loads:
         load.wait()
     with jax.named_scope("permute"):
@@ -259,18 +271,24 @@
         for kind, partner in ((0, nxt), (1, prv)):
             xs = column(kind, dx)
 
-            @pl.loop(0, SIDE // 2)
-            def _(t):
+            def send_on(t, sem):
                 ys = mod(y + SIDE - t, SIDE) if kind == 0 else mod(y + t, SIDE)
                 source = xs * SIDE + ys
                 pltpu.make_async_remote_copy(
                     src_ref=raw.at[kind, source],
                     dst_ref=raw.at[1 - kind, source],
-                    send_sem=sent_sem.at[1],
+                    send_sem=sent_sem.at[sem],
                     recv_sem=relay_sem.at[1 - kind, dx],
                     device_id={"genes": partner},
                     device_id_type=MESH,
                 ).start()
+
+            for t in (0, 2, 3):
+                send_on(t, 1)
+
+            @pl.when(y != (SIDE - 1 if kind == 0 else 0))
+            def _():
+                send_on(1, 3 + kind)
 
     def slots_of(kind, xs):
         at = pl.ds(xs * SIDE, SIDE)
@@ -327,41 +345,21 @@
     def _(i):
         pass_on(i, 0)
 
+    @pl.loop(SIDE // 2, SIDE)
+    def _(i):
+        pass_on(i)
+
     expr_copy.wait()
 
     def pair_out(p):
         panel_chunk(chunk(2 * p))
         panel_chunk(chunk(2 * p + 1))
 
-    @pl.loop(2, SIDE // 2)
-    def _(p):
-        pass_on(2 * p)
-        pass_on(2 * p + 1)
-        with jax.named_scope("ratio"):
-            ratio_pair(p - 2)
-
+    with jax.named_scope("ratio"):
+        ratio_pair(0)
+    with jax.named_scope("ratio"):
+        ratio_pair(1)
     pair_out(0)
-    pair_out(1)
-    for p in (2, 3):
-        with jax.named_scope("ratio_end"):
-            ratio_pair(p)
-        if p > 2:
-            pair_out(p - 1)
-
-    def joined(kind, slot):
-        return jnp.concatenate([panel[kind, slot, k] for k in range(SIDE)], axis=1)
-
-    first_left = joined(core, 0)
-    pair_out(SIDE // 2 - 1)
-    with jax.named_scope("partial"):
-
-        @pl.loop(0, HALF // STEP)
-        def _(c):
-            at = pl.multiple_of(c * STEP, STEP)
-            partial[c] = lax.dot_general(
-                first_left, dose[0, pl.ds(at, STEP)], NT, preferred_element_type=jnp.float32
-            )
-
     with jax.named_scope("dose_wait"):
         dose_copy.wait_recv()
     with jax.named_scope("squares_1"):
@@ -370,6 +368,9 @@
         def _(i):
             dose_squares(1, i * 512, 512)
 
+    pair_out(1)
+    with jax.named_scope("ratio_end"):
+        ratio_pair(2)
     count = float(2 * HALF)
     with jax.named_scope("square_rows"):
         for c in range(W // 512):
@@ -381,6 +382,26 @@
                 precision=lax.Precision.HIGHEST,
                 preferred_element_type=jnp.float32,
             )
+
+    pair_out(2)
+    with jax.named_scope("ratio_end"):
+        ratio_pair(3)
+
+    def joined(kind, slot):
+        return jnp.concatenate([panel[kind, slot, k] for k in range(SIDE)], axis=1)
+
+    first_left = joined(core, 0)
+    pair_out(SIDE // 2 - 1)
+    with jax.named_scope("partial"):
+
+        @pl.loop(0, HALF // STEP)
+        def _(c):
+            at = pl.multiple_of(c * STEP, STEP)
+            product = lax.dot_general(
+                first_left, dose[0, pl.ds(at, STEP)], NT, preferred_element_type=jnp.float32
+            )
+            for k in range(STEP // ALIGN):
+                partial[c * (STEP // ALIGN) + k] = product[:, k * ALIGN : (k + 1) * ALIGN]
 
     def panel_wait(kind, way):
         pltpu.make_async_copy(panel.at[kind, 1], panel.at[kind, 1], panel_sem.at[kind, way]).wait()
@@ -413,17 +434,17 @@
         left = joined(kind, 1)
         base = None if first == 0 else joined(kind, 0)
 
-        @pl.loop(0, HALF // STEP)
+        step = STEP if after is None else ALIGN
+
+        @pl.loop(0, HALF // step)
         def _(c):
-            at = pl.multiple_of(first + c * STEP, STEP)
+            at = pl.multiple_of(first + c * step, step)
             product = lax.dot_general(
-                left, dose[1, pl.ds(at, STEP)], NT, preferred_element_type=jnp.float32
+                left, dose[1, pl.ds(at, step)], NT, preferred_element_type=jnp.float32
             )
-            if base is None:
-                product = product + partial[c]
-            else:
+            if base is not None:
                 product = product + lax.dot_general(
-                    base, dose[0, pl.ds(at, STEP)], NT, preferred_element_type=jnp.float32
+                    base, dose[0, pl.ds(at, step)], NT, preferred_element_type=jnp.float32
                 )
             if after is not None:
 
@@ -431,26 +452,28 @@
                 def _():
                     after(c - 1)
 
-            for k in range(STEP // ALIGN):
+            for k in range(step // ALIGN):
+                tile = c * (step // ALIGN) + k
                 here = pl.ds(pl.multiple_of(at + k * ALIGN, ALIGN), ALIGN)
                 part = product[:, k * ALIGN : (k + 1) * ALIGN]
+                if base is None:
+                    part = part + partial[tile]
                 total = part[USED : USED + 1]
                 mean = total * (1.0 / count)
                 dev = lax.rsqrt(jnp.maximum(stat[0:1, here] - total * mean, 1.0)) * scale
                 part = (part - pstat[0] * mean) * dev * pstat[1]
-                to_ref[c * (STEP // ALIGN) + k] = part.astype(jnp.bfloat16)
+                to_ref[tile] = part.astype(jnp.bfloat16)
         if after is not None:
-            after(HALF // STEP - 1)
+            after(HALF // step - 1)
 
     keep = jnp.where(me == 0, 0.0, 1.0)
 
-    per = STEP // ALIGN
     first_half, second_half = z_ref.at[0:SIDE], z_ref.at[SIDE : 2 * SIDE]
 
     def give(c):
         return pltpu.make_async_remote_copy(
-            src_ref=back.at[pl.ds(c * per, per)],
-            dst_ref=land.at[pl.ds(c * per, per)],
+            src_ref=back.at[c],
+            dst_ref=land.at[c],
             send_sem=back_send_sem,
             recv_sem=back_sem.at[c],
             device_id={"genes": prv},
@@ -477,37 +500,32 @@
 
     gene = lax.broadcasted_iota(jnp.int32, (ROWS, ALIGN), 0) & (GENE_DEV - 1)
 
-    def write(c):
-        to = pl.ds(pl.multiple_of(c * STEP, STEP), STEP)
-        return pltpu.make_async_copy(result.at[c], out_ref.at[:, :, to], out_sem.at[c])
+    def write(m):
+        to = pl.ds(pl.multiple_of(m * ALIGN, ALIGN), ALIGN)
+        return pltpu.make_async_copy(result.at[m], out_ref.at[:, :, to], out_sem.at[m])
 
     with jax.named_scope("cut"):
 
-        @pl.loop(0, HALF // STEP)
-        def _(c):
+        @pl.loop(0, SIDE)
+        def _(m):
             @pl.when(core == 1)
             def _():
-                piece = land.at[pl.ds(c * per, per)]
-                pltpu.make_async_copy(piece, piece, back_sem.at[c]).wait()
-                for k in range(per):
-                    z_ref[SIDE + c * per + k] = land[c * per + k]
-
-            for k in range(per):
-                part = None
-                for g in range(GENE_DEV):
-                    value = z_ref[lax.shift_right_logical(start_ref[g], 7) + (c * per + k)]
-                    part = value if g == 0 else jnp.where(gene == g, value, part)
-                result[c, :, :, k * ALIGN : (k + 1) * ALIGN] = part[:USED].reshape(
-                    PHEN, GENE_DEV, ALIGN
-                )
-
-            @pl.when(c > 0)
+                pltpu.make_async_copy(land.at[m], land.at[m], back_sem.at[m]).wait()
+                z_ref[SIDE + m] = land[m]
+
+            part = None
+            for g in range(GENE_DEV):
+                value = z_ref[lax.shift_right_logical(start_ref[g], 7) + m]
+                part = value if g == 0 else jnp.where(gene == g, value, part)
+            result[m] = part[:USED].reshape(PHEN, GENE_DEV, ALIGN)
+
+            @pl.when(m > 0)
             def _():
-                write(c - 1).start()
-
-        write(HALF // STEP - 1).start()
-        for c in range(HALF // STEP):
-            write(c).wait()
+                write(m - 1).start()
+
+        write(SIDE - 1).start()
+        for m in range(SIDE):
+            write(m).wait()
 
     @pl.when(core == 1)
     def _():
@@ -515,7 +533,15 @@
 
     dose_copy.wait_send()
     pltpu.make_async_copy(raw.at[0, 0 : n - 2], raw.at[0, 0 : n - 2], sent_sem.at[0]).wait()
-    pltpu.make_async_copy(raw.at[0], raw.at[0], sent_sem.at[1]).wait()
+    most = raw.at[0, 0 : n - 2 * SIDE]
+    pltpu.make_async_copy(most, most, sent_sem.at[1]).wait()
+    for sem, there in ((2, inside), (3, y != SIDE - 1), (4, y != 0)):
+
+        @pl.when(there)
+        def _():
+            few = raw.at[0, 0:SIDE]
+            pltpu.make_async_copy(few, few, sent_sem.at[sem]).wait()
+
     panel_wait(0, 0)
 
     @pl.when(core == 0)
@@ -551,18 +577,18 @@
             pltpu.VMEM((2, 2 * RATIOS, LANES), bf16),
             pltpu.VMEM((SIDE, ROWS, ALIGN), bf16),
             pltpu.VMEM((SIDE, ROWS, ALIGN), bf16),
-            pltpu.VMEM((HALF // STEP, ROWS, STEP), f32),
-            pltpu.VMEM((HALF // STEP, PHEN, GENE_DEV, STEP), bf16),
+            pltpu.VMEM((SIDE, ROWS, ALIGN), f32),
+            pltpu.VMEM((SIDE, PHEN, GENE_DEV, ALIGN), bf16),
             dma((2, SIDE)),
             dma((2, SIDE)),
             dma((2, 2)),
-            dma((2,)),
+            dma((5,)),
             dma,
             dma((2,)),
             dma((2,)),
-            dma((HALF // STEP,)),
+            dma((SIDE,)),
             dma,
-            dma((HALF // STEP,)),
+            dma((SIDE,)),
             dma((6,)),
         ],
         compiler_params=pltpu.CompilerParams(collective_id=0, has_side_effects=True),

time: 61.3 us -> 58.3 us (0.951)
  Pallas kernels: 59.2 us -> 56.2 us
    pallas_call x1, Pallas kernels: 59.2 us -> 56.2 us  [shards(): pl.pallas_call(functools.partial(kernel, n), out_shape=jax.ShapeDtypeStru...]
where the time goes in v6:
time: 58.3 us; the launch traced here: 58.2 us
  Pallas kernels  56.2 us (96%)
  local copies, waits for them, and re-layouts  1.98 us (3%)
    pallas_call x1, Pallas kernels, shards(): pl.pallas_call(functools.partial(kernel, n), out_shape=jax.ShapeDtypeStru...  56.2 us
    unnamed x1, local copies, waits for them, and re-layouts  1.98 us

profile of v6, /device:TPU:513, one launch (start us, length us, event | category | flops | bytes accessed | tf_op | source)
XLA Modules:
  0.0 58.2 jit_solution(10492353365758359934)
XLA Ops:
  0.0 56.2 %associate.1 = bf16[41,8,1024]{2,1,0:T(8,128)(2,1)} custom-call(s32[512]{0:T(512)} %block_hbm.1, s32[8]{0:T(128)} %start_hbm.1, bf16[16,20480]{1,0:T(8,128)(2,1)} %counts_hbm.1, bf16[8,1024]{1,0:T(8,128)(2,1)} %expr_ref.1, s32[8,512]{1,0:T(8,128)} %bitcast.5, s32[40,512]{1,0:T(8,128)} %bitcast.4, bf16[2048,1024]{1,0:T(8,128)(2,1)} %dose_ref.1), custom_call_target="tpu_custom_call" | custom-call | tf_op jit(solution)/shard_map/associate/pallas_call | solution.py:556
  56.2 2.0 %copy.9 = bf16[8,41,1024]{2,0,1:T(8,128)(2,1)} copy(bf16[8,41,1024]{2,0,1:T(8,128)(2,1)} %bitcast.3) | data formatting | bytes 1343488

commit v7 on v6

--- a/solution.py
+++ b/solution.py
@@ -120,7 +120,6 @@
     sd,
     back,
     land,
-    partial,
     result,
     direct_sem,
     relay_sem,
@@ -133,6 +132,7 @@
     back_send_sem,
     out_sem,
     load_sem,
+    whole_sem,
 ):
     me = lax.axis_index("genes")
     core = lax.axis_index("samples")
@@ -160,54 +160,64 @@
     barrier = pltpu.get_barrier_semaphore()
     pl.semaphore_signal(barrier, inc=1, device_id={"samples": other}, device_id_type=MESH)
 
+    @pl.when(core == 1)
+    def _():
+        pl.semaphore_signal(
+            barrier, inc=1, device_id={"genes": nxt, "samples": 0}, device_id_type=MESH
+        )
+
     @pl.loop(1, n)
     def _(step):
         pl.semaphore_signal(
             barrier, inc=1, device_id={"genes": mod(me + step, n)}, device_id_type=MESH
         )
 
-    mine = pltpu.make_async_copy(dose_ref, dose.at[0], local_sem)
+    mine = pltpu.make_async_copy(
+        dose_ref.at[pl.ds(pl.multiple_of(core * HALF, HALF), HALF)], dose.at[0], local_sem
+    )
     mine.start()
 
     def chunk(i):
         half = lax.shift_right_logical(i + 1, 1)
         return jnp.where((i & 1) == 1, half, mod(SIDE - half, SIDE))
 
+    def message(owner, kind, dest, send, recv):
+        return pltpu.make_async_remote_copy(
+            src_ref=msgs.at[owner],
+            dst_ref=raw.at[kind, me],
+            send_sem=sent_sem.at[send],
+            recv_sem=recv,
+            device_id={"genes": dest},
+            device_id_type=MESH,
+        )
+
     def send_chunk(dx):
-        @pl.loop(0, SIDE, unroll=4)
-        def _(yo):
-            owner = mod(x + dx, SIDE) * SIDE + yo
-            near = mod(yo - y + SIDE, SIDE) < SIDE // 2
-            kind = jnp.where(near, 0, 1)
-            dest = jnp.where(near, owner, mod(owner + 1, n))
-
-            @pl.when(dest != me)
-            def _():
-                pltpu.make_async_remote_copy(
-                    src_ref=msgs.at[owner],
-                    dst_ref=raw.at[kind, me],
-                    send_sem=sent_sem.at[0],
-                    recv_sem=direct_sem.at[kind, dx],
-                    device_id={"genes": dest},
-                    device_id_type=MESH,
-                ).start()
-
-            @pl.when(dest == me)
-            def _():
-                pltpu.make_async_copy(
-                    msgs.at[owner], raw.at[kind, me], direct_sem.at[kind, dx]
-                ).start()
-
-            @pl.when((yo == SIDE - 1) & inside)
-            def _():
-                pltpu.make_async_remote_copy(
-                    src_ref=msgs.at[owner],
-                    dst_ref=raw.at[1 - kind, me],
-                    send_sem=sent_sem.at[2],
-                    recv_sem=relay_sem.at[1 - kind, dx],
-                    device_id={"genes": jnp.where(near, mod(owner + 1, n), owner)},
-                    device_id_type=MESH,
-                ).start()
+        row = mod(x + dx, SIDE) * SIDE
+        for delta in range(SIDE):
+            owner = row + mod(y + delta, SIDE)
+            after = mod(owner + 1, n)
+            near = delta < SIDE // 2
+            kind, dest, twin = (0, owner, after) if near else (1, after, owner)
+            give = message(owner, kind, dest, 0, direct_sem.at[kind, dx])
+            if delta in (0, SIDE - 1):
+
+                @pl.when(dest != me)
+                def _():
+                    give.start()
+
+                @pl.when(dest == me)
+                def _():
+                    pltpu.make_async_copy(
+                        msgs.at[owner], raw.at[kind, me], direct_sem.at[kind, dx]
+                    ).start()
+
+            else:
+                give.start()
+            if delta in (1, SIDE - 2):
+
+                @pl.when(y == SIDE - 1 - delta)
+                def _():
+                    message(owner, 1 - kind, twin, 2, relay_sem.at[1 - kind, dx]).start()
 
     for load in loads:
         load.wait()
@@ -221,7 +231,7 @@
             permuted(counts_ref, block_ref, msgs, owner)
 
     with jax.named_scope("barrier"):
-        pl.semaphore_wait(barrier, n)
+        pl.semaphore_wait(barrier, n + 1 - core)
     expr_copy = pltpu.make_async_remote_copy(
         src_ref=expr_ref,
         dst_ref=expr.at[1],
@@ -238,7 +248,7 @@
             send_chunk(chunk(i))
 
     dose_copy = pltpu.make_async_remote_copy(
-        src_ref=dose_ref,
+        src_ref=dose_ref.at[pl.ds(pl.multiple_of(other * HALF, HALF), HALF)],
         dst_ref=dose.at[1],
         send_sem=dose_sem.at[0],
         recv_sem=dose_sem.at[1],
@@ -328,16 +338,16 @@
         )
 
     def panel_chunk(dx):
-        panel_copy(0, dx).start()
-
-        @pl.when(core == 0)
+        @pl.when(core == 1)
         def _():
             panel_copy(1, dx).start()
+
+        panel_copy(0, dx).start()
 
     def pass_on(i, slot=None):
         if slot is not None:
             with jax.named_scope("squares"):
-                dose_squares(slot, i * 512, 512)
+                dose_squares(slot, i * STEP, STEP)
         with jax.named_scope("relay"):
             relay_chunk(chunk(i))
 
@@ -364,16 +374,16 @@
         dose_copy.wait_recv()
     with jax.named_scope("squares_1"):
 
-        @pl.loop(0, W // 512)
+        @pl.loop(0, HALF // STEP)
         def _(i):
-            dose_squares(1, i * 512, 512)
+            dose_squares(1, i * STEP, STEP)
 
     pair_out(1)
     with jax.named_scope("ratio_end"):
         ratio_pair(2)
     count = float(2 * HALF)
     with jax.named_scope("square_rows"):
-        for c in range(W // 512):
+        for c in range(HALF // 512):
             at = slice(c * 512, (c + 1) * 512)
             stat[:, at] = lax.dot_general(
                 jnp.ones((8, ALIGN), jnp.float32),
@@ -390,62 +400,45 @@
     def joined(kind, slot):
         return jnp.concatenate([panel[kind, slot, k] for k in range(SIDE)], axis=1)
 
-    first_left = joined(core, 0)
     pair_out(SIDE // 2 - 1)
-    with jax.named_scope("partial"):
-
-        @pl.loop(0, HALF // STEP)
-        def _(c):
-            at = pl.multiple_of(c * STEP, STEP)
-            product = lax.dot_general(
-                first_left, dose[0, pl.ds(at, STEP)], NT, preferred_element_type=jnp.float32
-            )
-            for k in range(STEP // ALIGN):
-                partial[c * (STEP // ALIGN) + k] = product[:, k * ALIGN : (k + 1) * ALIGN]
+
+    PIECE = 48
+
+    def pheno_sums(kind, slot):
+        for g in range(ROWS // PIECE):
+            rows = slice(g * PIECE, (g + 1) * PIECE)
+            total = jnp.zeros((PIECE, ALIGN), jnp.float32) if slot == 0 else pstat[0, rows]
+            square = jnp.zeros((PIECE, ALIGN), jnp.float32) if slot == 0 else pstat[1, rows]
+            for k in range(SIDE):
+                value = panel[kind, slot, k, rows].astype(jnp.float32)
+                total = total + value
+                square = square + value * value
+            if slot == 1:
+                total = jnp.sum(total, axis=1, keepdims=True)
+                square = jnp.sum(square, axis=1, keepdims=True)
+                square = lax.rsqrt(jnp.maximum(square - total * total / count, 1.0))
+            pstat[0, rows] = jnp.broadcast_to(total, (PIECE, ALIGN))
+            pstat[1, rows] = jnp.broadcast_to(square, (PIECE, ALIGN))
+
+    pheno_sums(1 - core, 0)
 
     def panel_wait(kind, way):
         pltpu.make_async_copy(panel.at[kind, 1], panel.at[kind, 1], panel_sem.at[kind, way]).wait()
 
-    with jax.named_scope("panel_wait"):
-        panel_wait(0, 1)
-
-    @pl.when(core == 1)
-    def _():
-        panel_wait(1, 1)
-
-    def pheno_stats(kind):
-        PIECE = 48
-        for g in range(ROWS // PIECE):
-            rows = slice(g * PIECE, (g + 1) * PIECE)
-            total = jnp.zeros((PIECE, ALIGN), jnp.float32)
-            square = jnp.zeros((PIECE, ALIGN), jnp.float32)
-            for slot in range(2):
-                for k in range(SIDE):
-                    value = panel[kind, slot, k, rows].astype(jnp.float32)
-                    total = total + value
-                    square = square + value * value
-            total = jnp.sum(total, axis=1, keepdims=True)
-            square = jnp.sum(square, axis=1, keepdims=True)
-            pstat[0, rows] = jnp.broadcast_to(total, (PIECE, ALIGN))
-            scale = lax.rsqrt(jnp.maximum(square - total * total / count, 1.0))
-            pstat[1, rows] = jnp.broadcast_to(scale, (PIECE, ALIGN))
-
-    def assoc(kind, first, to_ref, scale, after=None):
+    def assoc(kind, to_ref, scale, after=None):
         left = joined(kind, 1)
-        base = None if first == 0 else joined(kind, 0)
+        base = joined(kind, 0)
 
         step = STEP if after is None else ALIGN
 
         @pl.loop(0, HALF // step)
         def _(c):
-            at = pl.multiple_of(first + c * step, step)
+            at = pl.multiple_of(c * step, step)
             product = lax.dot_general(
                 left, dose[1, pl.ds(at, step)], NT, preferred_element_type=jnp.float32
+            ) + lax.dot_general(
+                base, dose[0, pl.ds(at, step)], NT, preferred_element_type=jnp.float32
             )
-            if base is not None:
-                product = product + lax.dot_general(
-                    base, dose[0, pl.ds(at, step)], NT, preferred_element_type=jnp.float32
-                )
             if after is not None:
 
                 @pl.when(c > 0)
@@ -456,8 +449,6 @@
                 tile = c * (step // ALIGN) + k
                 here = pl.ds(pl.multiple_of(at + k * ALIGN, ALIGN), ALIGN)
                 part = product[:, k * ALIGN : (k + 1) * ALIGN]
-                if base is None:
-                    part = part + partial[tile]
                 total = part[USED : USED + 1]
                 mean = total * (1.0 / count)
                 dev = lax.rsqrt(jnp.maximum(stat[0:1, here] - total * mean, 1.0)) * scale
@@ -476,27 +467,43 @@
             dst_ref=land.at[c],
             send_sem=back_send_sem,
             recv_sem=back_sem.at[c],
-            device_id={"genes": prv},
+            device_id={"genes": prv, "samples": 1},
             device_id_type=MESH,
         )
 
+    whole = pltpu.make_async_remote_copy(
+        src_ref=first_half,
+        dst_ref=second_half,
+        send_sem=whole_sem.at[0],
+        recv_sem=whole_sem.at[1],
+        device_id={"samples": 0},
+        device_id_type=MESH,
+    )
+
     @pl.when(core == 0)
     def _():
+        with jax.named_scope("panel_wait"):
+            panel_wait(1, 1)
         with jax.named_scope("pstats_a"):
-            pheno_stats(0)
+            pheno_sums(1, 1)
         with jax.named_scope("assoc_a"):
-            assoc(0, 0, first_half, 1.0)
-            assoc(0, HALF, second_half, 1.0)
+            assoc(1, back, keep, lambda c: give(c).start())
+        with jax.named_scope("assoc_b"):
+            panel_wait(0, 1)
+            pheno_sums(0, 0)
+            pheno_sums(0, 1)
+            assoc(0, first_half, 1.0)
+            whole.wait_recv()
 
     @pl.when(core == 1)
     def _():
+        with jax.named_scope("panel_wait"):
+            panel_wait(0, 1)
         with jax.named_scope("pstats_b"):
-            pheno_stats(1)
-        with jax.named_scope("assoc_b"):
-            assoc(1, 0, back, keep, lambda c: give(c).start())
+            pheno_sums(0, 1)
         with jax.named_scope("assoc_c"):
-            pheno_stats(0)
-            assoc(0, HALF, first_half, 1.0)
+            assoc(0, first_half, 1.0)
+            whole.start()
 
     gene = lax.broadcasted_iota(jnp.int32, (ROWS, ALIGN), 0) & (GENE_DEV - 1)
 
@@ -527,7 +534,7 @@
         for m in range(SIDE):
             write(m).wait()
 
-    @pl.when(core == 1)
+    @pl.when(core == 0)
     def _():
         pltpu.make_async_copy(back, back, back_send_sem).wait()
 
@@ -544,9 +551,32 @@
 
     panel_wait(0, 0)
 
-    @pl.when(core == 0)
+    @pl.when(core == 1)
     def _():
+        whole.wait_send()
         panel_wait(1, 0)
+
+
+def finish(in_ref, out_ref, held, in_sem, out_sem):
+    pieces = held.shape[0]
+    rows = in_ref.shape[0]
+    most = held.shape[1]
+    spans = [(k * most, min(most, rows - k * most)) for k in range(pieces)]
+    takes = [
+        pltpu.make_async_copy(in_ref.at[at : at + size], held.at[k, 0:size], in_sem.at[k])
+        for k, (at, size) in enumerate(spans)
+    ]
+    gives = [
+        pltpu.make_async_copy(held.at[k, 0:size], out_ref.at[at : at + size], out_sem.at[k])
+        for k, (at, size) in enumerate(spans)
+    ]
+    for take in takes:
+        take.start()
+    for take, give in zip(takes, gives):
+        take.wait()
+        give.start()
+    for give in gives:
+        give.wait()
 
 
 def shards(dosage, expression, intron_counts, cluster_sizes, valid_mask, gene_block, window_start):
@@ -570,14 +600,13 @@
             pltpu.VMEM((2, n, SLOTS, ALIGN), bf16),
             pltpu.VMEM((2, GENE_DEV, HALF), bf16),
             pltpu.VMEM((2, 2, SIDE, ROWS, ALIGN), bf16),
-            pltpu.VMEM((2, W, HALF), bf16),
-            pltpu.VMEM((W, ALIGN), f32),
-            pltpu.VMEM((8, W), f32),
+            pltpu.VMEM((2, HALF, HALF), bf16),
+            pltpu.VMEM((HALF, ALIGN), f32),
+            pltpu.VMEM((8, HALF), f32),
             pltpu.VMEM((2, ROWS, ALIGN), f32),
             pltpu.VMEM((2, 2 * RATIOS, LANES), bf16),
             pltpu.VMEM((SIDE, ROWS, ALIGN), bf16),
             pltpu.VMEM((SIDE, ROWS, ALIGN), bf16),
-            pltpu.VMEM((SIDE, ROWS, ALIGN), f32),
             pltpu.VMEM((SIDE, PHEN, GENE_DEV, ALIGN), bf16),
             dma((2, SIDE)),
             dma((2, SIDE)),
@@ -590,6 +619,7 @@
             dma,
             dma((SIDE,)),
             dma((6,)),
+            dma((2,)),
         ],
         compiler_params=pltpu.CompilerParams(collective_id=0, has_side_effects=True),
         name="associate",
@@ -602,6 +632,15 @@
         valid_mask.T,
         dosage,
     )
+    pieces, most = 4, -(-PHEN // 4)
+    out = pl.pallas_call(
+        finish,
+        out_shape=jax.ShapeDtypeStruct(out.shape, out.dtype),
+        in_specs=[pl.BlockSpec(memory_space=pl.ANY)],
+        out_specs=pl.BlockSpec(memory_space=pl.ANY),
+        scratch_shapes=[pltpu.VMEM((pieces, most, GENE_DEV, HALF), bf16), dma((pieces,)), dma((pieces,))],
+        name="finish",
+    )(out)
     return jnp.swapaxes(out, 0, 1)
 
 

time: 58.3 us -> 57.3 us (0.983)
  local copies, waits for them, and re-layouts: 1.98 us -> 0 us
  Pallas kernels: 56.2 us -> 57.2 us
    unnamed x1 -> x0, local copies, waits for them, and re-layouts: 1.98 us -> none
    pallas_call x0 -> x1, Pallas kernels: none -> 1.9 us  [shards(): pl.pallas_call(finish, out_shape=jax.ShapeDtypeStruct(out.shape, out.dtyp...]
    pallas_call x1, Pallas kernels: 56.2 us -> 55.3 us  [shards(): pl.pallas_call(functools.partial(kernel, n), out_shape=jax.ShapeDtypeStru...]
where the time goes in v7:
time: 57.3 us; the launch traced here: 57.2 us
  Pallas kernels  57.2 us (100%)
    pallas_call x1, Pallas kernels, shards(): pl.pallas_call(functools.partial(kernel, n), out_shape=jax.ShapeDtypeStru...  55.3 us
    pallas_call x1, Pallas kernels, shards(): pl.pallas_call(finish, out_shape=jax.ShapeDtypeStruct(out.shape, out.dtyp...  1.9 us

profile of v7, /device:TPU:513, one launch (start us, length us, event | category | flops | bytes accessed | tf_op | source)
XLA Modules:
  0.0 57.2 jit_solution(2472501352024590716)
XLA Ops:
  0.0 55.3 %associate.1.in_ref = bf16[41,8,1024]{2,1,0:T(8,128)(2,1)} custom-call(s32[512]{0:T(512)} %block_hbm.1, s32[8]{0:T(128)} %start_hbm.1, bf16[16,20480]{1,0:T(8,128)(2,1)} %counts_hbm.1, bf16[8,1024]{1,0:T(8,128)(2,1)} %expr_ref.1, s32[8,512]{1,0:T(8,128)} %bitcast.4, s32[40,512]{1,0:T(8,128)} %bitcast.3, bf16[2048,1024]{1,0:T(8,128)(2,1)} %dose_ref.1), custom_call_target="tpu_custom_call" | custom-call | tf_op jit(solution)/shard_map/associate/pallas_call | solution.py:586
  55.3 1.9 %finish.1 = bf16[41,8,1024]{2,1,0:T(8,128)(2,1)} custom-call(bf16[41,8,1024]{2,1,0:T(8,128)(2,1)} %associate.1.in_ref), custom_call_target="tpu_custom_call" | custom-call | tf_op jit(solution)/shard_map/finish/pallas_call | solution.py:636

commit v8 on v7

--- a/solution.py
+++ b/solution.py
@@ -355,32 +355,16 @@
     def _(i):
         pass_on(i, 0)
 
+    with jax.named_scope("dose_wait"):
+        dose_copy.wait_recv()
+
     @pl.loop(SIDE // 2, SIDE)
     def _(i):
+        with jax.named_scope("squares_1"):
+            dose_squares(1, (i - SIDE // 2) * STEP, STEP)
         pass_on(i)
 
     expr_copy.wait()
-
-    def pair_out(p):
-        panel_chunk(chunk(2 * p))
-        panel_chunk(chunk(2 * p + 1))
-
-    with jax.named_scope("ratio"):
-        ratio_pair(0)
-    with jax.named_scope("ratio"):
-        ratio_pair(1)
-    pair_out(0)
-    with jax.named_scope("dose_wait"):
-        dose_copy.wait_recv()
-    with jax.named_scope("squares_1"):
-
-        @pl.loop(0, HALF // STEP)
-        def _(i):
-            dose_squares(1, i * STEP, STEP)
-
-    pair_out(1)
-    with jax.named_scope("ratio_end"):
-        ratio_pair(2)
     count = float(2 * HALF)
     with jax.named_scope("square_rows"):
         for c in range(HALF // 512):
@@ -393,9 +377,16 @@
                 preferred_element_type=jnp.float32,
             )
 
-    pair_out(2)
-    with jax.named_scope("ratio_end"):
-        ratio_pair(3)
+    def pair_out(p):
+        panel_chunk(chunk(2 * p))
+        panel_chunk(chunk(2 * p + 1))
+
+    with jax.named_scope("ratio"):
+        ratio_pair(0)
+    for p in range(1, SIDE // 2):
+        with jax.named_scope("ratio_end"):
+            ratio_pair(p)
+        pair_out(p - 1)
 
     def joined(kind, slot):
         return jnp.concatenate([panel[kind, slot, k] for k in range(SIDE)], axis=1)
@@ -436,8 +427,6 @@
             at = pl.multiple_of(c * step, step)
             product = lax.dot_general(
                 left, dose[1, pl.ds(at, step)], NT, preferred_element_type=jnp.float32
-            ) + lax.dot_general(
-                base, dose[0, pl.ds(at, step)], NT, preferred_element_type=jnp.float32
             )
             if after is not None:
 
@@ -445,6 +434,9 @@
                 def _():
                     after(c - 1)
 
+            product = product + lax.dot_general(
+                base, dose[0, pl.ds(at, step)], NT, preferred_element_type=jnp.float32
+            )
             for k in range(step // ALIGN):
                 tile = c * (step // ALIGN) + k
                 here = pl.ds(pl.multiple_of(at + k * ALIGN, ALIGN), ALIGN)

time: 57.3 us -> 56.9 us (level)
  no operation moved by 1% of the time
where the time goes in v8:
time: 56.9 us; the launch traced here: 56.7 us
  Pallas kernels  56.7 us (100%)
    pallas_call x1, Pallas kernels, shards(): pl.pallas_call(functools.partial(kernel, n), out_shape=jax.ShapeDtypeStru...  54.8 us
    pallas_call x1, Pallas kernels, shards(): pl.pallas_call(finish, out_shape=jax.ShapeDtypeStruct(out.shape, out.dtyp...  1.9 us

profile of v8, /device:TPU:513, one launch (start us, length us, event | category | flops | bytes accessed | tf_op | source)
XLA Modules:
  0.0 56.7 jit_solution(4052127374185046052)
XLA Ops:
  0.0 54.8 %associate.1.in_ref = bf16[41,8,1024]{2,1,0:T(8,128)(2,1)} custom-call(s32[512]{0:T(512)} %block_hbm.1, s32[8]{0:T(128)} %start_hbm.1, bf16[16,20480]{1,0:T(8,128)(2,1)} %counts_hbm.1, bf16[8,1024]{1,0:T(8,128)(2,1)} %expr_ref.1, s32[8,512]{1,0:T(8,128)} %bitcast.4, s32[40,512]{1,0:T(8,128)} %bitcast.3, bf16[2048,1024]{1,0:T(8,128)(2,1)} %dose_ref.1), custom_call_target="tpu_custom_call" | custom-call | tf_op jit(solution)/shard_map/associate/pallas_call | solution.py:578
  54.8 1.9 %finish.1 = bf16[41,8,1024]{2,1,0:T(8,128)(2,1)} custom-call(bf16[41,8,1024]{2,1,0:T(8,128)(2,1)} %associate.1.in_ref), custom_call_target="tpu_custom_call" | custom-call | tf_op jit(solution)/shard_map/finish/pallas_call | solution.py:628
